TPU v7x, 1024 devices: a whole 4x4x32 slice. The times are simulated.
1024 devices in a mesh: gz: 16 (over x, y), gy: 64 (over z, core).
Axes of the slice: x: 4, y: 4, z: 32, core: 2. Of those that a mesh axis runs over, the one named last changes fastest.
Arguments:
- grid_grad: float32 [256, 1024, 512], P('gz', 'gy'), may hold values from -6 to 6
- cells: int32 [3, 2097152], P(None, ('gz', 'gy')), may hold values from 0 to 1023, as said below
- offsets: int32 [3, 2097152], P(None, ('gz', 'gy')), may hold values from 0 to 1023
- owners: int32 [2097152, 1], P(('gz', 'gy')), may hold values from 0 to 1023; in each aligned block of 2048 rows (0 to 2047, 2048 to 4095, ...) at most 4 rows name the same one
- slots: int32 [2097152], P(('gz', 'gy')), may hold values from 0 to 2047
Outputs:
- pos_grad: float32 [3, 2097152], P(None, ('gz', 'gy'))
Inputs may be any that keep to these rules, and one draw needn't show every extreme that they name: `cells`: the row's cell lies in the mesh block of the device that holds the row: along z in [gz * 16, gz * 16 + 16), along y in [gy * 16, gy * 16 + 16), where gz, gy are that device's indices. `owners`: owners are linear device indices gz * 64 + gy. Among the rows of one device, no owner is named by more than 4 rows; some owner is named by exactly 4.
All inputs are finite; a program needn't handle non-finite values.
Results may differ from a plain program's by a relative error of at most 0.0003.
Values sent between devices are 32-bit elements; how exact they have to be, the bound alone decides.
No kernel may reach another device: no remote copies, remote signals or barrier semaphores. Data moves between devices by JAX's collectives and lax.ppermute only.
A program may use at most 32 MiB of HBM per device.

v0:
```python
import jax
import jax.numpy as jnp
from jax import lax
from jax.sharding import PartitionSpec as P


def from_behind(block, axis, distance):
    devices = range(lax.axis_size(axis))
    route = [((i - distance) % len(devices), i) for i in devices]
    return lax.ppermute(block, axis, route)


def two_weights(index, frac, length):
    places = lax.broadcasted_iota(jnp.int32, (index.shape[0], length), 1)
    lower = (places == index[:, None]).astype(jnp.float32)
    upper = (places == ((index + 1) % length)[:, None]).astype(jnp.float32)
    weights = lower * (1.0 - frac)[:, None] + upper * frac[:, None]
    return (weights, upper - lower)


def body(grid_grad, cells, offsets, owners, slots):
    block_z, block_y, size_x = grid_grad.shape
    upper_z = from_behind(grid_grad[:1], "gz", -1)
    with_z = jnp.concatenate([grid_grad, upper_z], axis=0)
    upper_y = from_behind(with_z[:, :1], "gy", -1)
    extended = jnp.concatenate([with_z, upper_y], axis=1)
    ext_z = block_z + 1
    ext_y = block_y + 1
    plane = extended.reshape(ext_z * ext_y, size_x)
    local_z = cells[0] - lax.axis_index("gz") * block_z
    local_y = cells[1] - lax.axis_index("gy") * block_y
    fraction = (offsets.astype(jnp.float32) + 0.5) / 1024.0
    num_rows = cells.shape[1]
    rows_block = min(512, num_rows)
    num_blocks = num_rows // rows_block
    where_rows = jnp.stack([local_z, local_y, cells[2]])
    where_rows = where_rows.reshape(3, num_blocks, rows_block).transpose(1, 0, 2)
    frac_rows = fraction.reshape(3, num_blocks, rows_block).transpose(1, 0, 2)

    def read_block(carry, inputs):
        index, frac = inputs
        weight_x, diff_x = two_weights(index[2], frac[2], size_x)
        stacked = jnp.concatenate([weight_x, diff_x], axis=0)
        projected = lax.dot_general(
            stacked,
            plane,
            (((1,), (1,)), ((), ())),
            precision=lax.Precision.HIGHEST,
            preferred_element_type=jnp.float32,
        )
        projected = projected.reshape(2, index.shape[1], ext_z, ext_y)
        weight_z, diff_z = two_weights(index[0], frac[0], ext_z)
        weight_y, diff_y = two_weights(index[1], frac[1], ext_y)
        along_wy = jnp.sum(projected * weight_y[None, :, None, :], axis=3)
        along_dy = jnp.sum(projected[0] * diff_y[:, None, :], axis=2)
        grad_z = jnp.sum(along_wy[0] * diff_z, axis=1)
        grad_y = jnp.sum(along_dy * weight_z, axis=1)
        grad_x = jnp.sum(along_wy[1] * weight_z, axis=1)
        return (carry, jnp.stack([grad_z, grad_y, grad_x]))

    unused, read_out = lax.scan(read_block, 0, (where_rows, frac_rows))
    gradient = read_out.transpose(1, 0, 2).reshape(3, num_rows)
    count_z = lax.axis_size("gz")
    count_y = lax.axis_size("gy")
    devices_all = count_z * count_y
    capacity = 2 * num_rows // devices_all
    target = owners[:, 0]
    owner_hot = (
        target[:, None] == lax.broadcasted_iota(jnp.int32, (num_rows, devices_all), 1)
    ).astype(jnp.bfloat16)
    group = 128
    num_groups = num_rows // group
    grouped = owner_hot.reshape(num_groups, group, devices_all)
    lower_tri = (
        lax.broadcasted_iota(jnp.int32, (group, group), 0)
        > lax.broadcasted_iota(jnp.int32, (group, group), 1)
    ).astype(jnp.bfloat16)
    before = jnp.einsum("ij,gjd->gid", lower_tri, grouped, preferred_element_type=jnp.float32)
    group_counts = jnp.sum(grouped.astype(jnp.float32), axis=1)
    group_start = jnp.cumsum(group_counts, axis=0) - group_counts
    rank_float = jnp.sum(
        (before + group_start[:, None, :]) * grouped.astype(jnp.float32), axis=2
    ).reshape(num_rows)
    rank_int = rank_float.astype(jnp.int32)
    rank_hot = (
        rank_int[:, None] == lax.broadcasted_iota(jnp.int32, (num_rows, capacity), 1)
    ).astype(jnp.float32)
    values = jnp.concatenate([gradient, (slots + 1).astype(jnp.float32)[None]], axis=0)
    placed = jnp.einsum("cr,rk->ckr", values, rank_hot)
    send_all = jnp.einsum(
        "ckr,rd->ckd",
        placed,
        owner_hot.astype(jnp.float32),
        precision=lax.Precision.HIGHEST,
        preferred_element_type=jnp.float32,
    )
    send_grad = send_all[:3].reshape(3, capacity, count_z, count_y)
    slot_plus = send_all[3].astype(jnp.int32) - 1
    send_slot = jnp.where(slot_plus < 0, num_rows, slot_plus).reshape(1, capacity, count_z, count_y)
    recv_grad, recv_slot = (
        lax.all_to_all(
            lax.all_to_all(send_grad, "gz", split_axis=2, concat_axis=2, tiled=True),
            "gy",
            split_axis=3,
            concat_axis=3,
            tiled=True,
        ),
        lax.all_to_all(
            lax.all_to_all(send_slot, "gz", split_axis=2, concat_axis=2, tiled=True),
            "gy",
            split_axis=3,
            concat_axis=3,
            tiled=True,
        ),
    )
    recv_grad = recv_grad.reshape(3, -1)
    recv_slot = recv_slot.reshape(-1)
    received = recv_slot.shape[0]
    high_count = num_rows // 128
    slot_high = recv_slot // 128
    slot_low = recv_slot % 128
    high_hot = (
        slot_high[:, None] == lax.broadcasted_iota(jnp.int32, (received, high_count), 1)
    ).astype(jnp.float32)
    low_hot = (slot_low[:, None] == lax.broadcasted_iota(jnp.int32, (received, 128), 1)).astype(
        jnp.float32
    )
    spread = jnp.einsum("cm,mh->chm", recv_grad, high_hot)
    total = jnp.einsum(
        "chm,ml->chl",
        spread,
        low_hot,
        precision=lax.Precision.HIGHEST,
        preferred_element_type=jnp.float32,
    )
    return total.reshape(3, num_rows)


def solution(mesh):
    placed = (
        P("gz", "gy", None),
        P(None, ("gz", "gy")),
        P(None, ("gz", "gy")),
        P(("gz", "gy"), None),
        P(("gz", "gy")),
    )
    return jax.shard_map(
        body, mesh=mesh, in_specs=placed, out_specs=P(None, ("gz", "gy")), check_vma=False
    )
```

profile of v0, /device:TPU:1, one launch (start us, length us, event | category | flops | bytes accessed | tf_op | source)
XLA Modules:
  0.0 158.1 jit_solution(17738613646575248178)
XLA Ops:
  0.8 7.6 %collective-permute-start = (f32[1,16,512]{2,1,0:T(8,128)S(1)}, f32[1,16,512]{2,1,0:T(8,128)S(1)}, u32[]{:S(2)}, u32[]{:S(2)}) collective-permute-start(f32[1,16,512]{2,1,0:T(8,128)S(1)} %slice.94), channel_id=1, source_target_pairs={{64,0},{128,64},{192,128},{256,192},{320,256},{384,320},{448,384},... | collective-permute-start | bytes 98312 | tf_op jit(solution)/shard_map/ppermute | solution.py:10
  9.9 2.1 %convert_reduce_fusion = f32[16,1024]{1,0:T(8,128)S(1)} fusion(s32[16,128]{1,0:T(8,128)} %bitcast.133), kind=kLoop, calls=%fused_computation.44 | loop fusion | flops 8372224 | bytes 73728 | tf_op jit(solution)/shard_map/reduce_sum | solution.py:79
  12.1 4.8 %fusion.10 = f32[16,128]{1,0:T(8,128)S(1)} fusion(f32[16,1024]{1,0:T(8,128)S(1)} %sub.91, s32[16,128]{1,0:T(8,128)} %bitcast.134), kind=kOutput, calls=%fused_computation.45 | convolution fusion | flops 551565312 | bytes 81920 | tf_op jit(solution)/shard_map/ij,gjd->gid/dot_general | solution.py:78
  17.1 8.4 %collective-permute-start.1 = (f32[17,1,512]{2,1,0:T(1,128)S(1)}, f32[17,1,512]{2,1,0:T(1,128)S(1)}, u32[]{:S(2)}, u32[]{:S(2)}) collective-permute-start(f32[17,1,512]{2,1,0:T(1,128)S(1)} %slice.101), channel_id=1, source_target_pairs={{1,0},{2,1},{3,2},{4,3},{5,4},{6,5},{7,6},{8,7},{9,8},{10,9},{11,1... | collective-permute-start | bytes 104456 | tf_op jit(solution)/shard_map/ppermute | solution.py:10
  26.6 18.9 %while.13 = (s32[]{:T(128)}, f32[4,3,512]{2,1,0:T(4,128)S(1)}, s32[4,3,512]{2,1,0:T(4,128)S(1)}, f32[4,3,512]{2,1,0:T(4,128)S(1)}, f32[289,512]{1,0:T(8,128)S(1)}, /*index=5*/s32[]{:T(128)}, s32[]{:T(128)}, s32[]{}, s32[]{}) while((s32[]{:T(128)}, f32[4,3,512]{2,1,0:T(4,128)S(1)}, s32[4,3,512]{2,1,0:T(4,128)S(1)}, ...), condition=%wide.region_9.10_spmd, body=%wide.region_3.9_spmd.sunk | while | flops 1821921792 | bytes 13062289 | solution.py:61
  27.0 2.2 %fusion.50 = f32[1024,289]{0,1:T(8,128)S(1)} fusion(f32[289,512]{1,0:T(8,128)S(1)} %get-tuple-element.212, f32[512,512]{1,0:T(8,128)S(1)} %get-tuple-element.175, f32[512,512]{1,0:T(8,128)S(1)} %get-tuple-element.176), kind=kOutput, calls=%fused_computation.clone.1 | convolution fusion | flops 1818755072 | bytes 3872768 | tf_op jit(solution)/shard_map/while/body/eval_jaxpr/dot_general | solution.py:44
  29.7 1.0 reshape.352
  31.8 2.2 %fusion.50 = f32[1024,289]{0,1:T(8,128)S(1)} fusion(f32[289,512]{1,0:T(8,128)S(1)} %get-tuple-element.212, f32[512,512]{1,0:T(8,128)S(1)} %get-tuple-element.175, f32[512,512]{1,0:T(8,128)S(1)} %get-tuple-element.176), kind=kOutput, calls=%fused_computation.clone.1 | convolution fusion | flops 1818755072 | bytes 3872768 | tf_op jit(solution)/shard_map/while/body/eval_jaxpr/dot_general | solution.py:44
  34.4 1.0 reshape.352
  36.5 2.2 %fusion.50 = f32[1024,289]{0,1:T(8,128)S(1)} fusion(f32[289,512]{1,0:T(8,128)S(1)} %get-tuple-element.212, f32[512,512]{1,0:T(8,128)S(1)} %get-tuple-element.175, f32[512,512]{1,0:T(8,128)S(1)} %get-tuple-element.176), kind=kOutput, calls=%fused_computation.clone.1 | convolution fusion | flops 1818755072 | bytes 3872768 | tf_op jit(solution)/shard_map/while/body/eval_jaxpr/dot_general | solution.py:44
  39.1 1.0 reshape.352
  41.2 2.2 %fusion.50 = f32[1024,289]{0,1:T(8,128)S(1)} fusion(f32[289,512]{1,0:T(8,128)S(1)} %get-tuple-element.212, f32[512,512]{1,0:T(8,128)S(1)} %get-tuple-element.175, f32[512,512]{1,0:T(8,128)S(1)} %get-tuple-element.176), kind=kOutput, calls=%fused_computation.clone.1 | convolution fusion | flops 1818755072 | bytes 3872768 | tf_op jit(solution)/shard_map/while/body/eval_jaxpr/dot_general | solution.py:44
  43.8 1.0 reshape.352
  45.5 2.9 %fusion.14 = f32[4,4,1024]{2,1,0:T(4,128)S(1)} fusion(s32[2048]{0:T(1024)S(1)} %bitcast.135, f32[2048,4]{0,1:T(4,128)S(1)} %maximum_bitcast_fusion.1, f32[2048,4]{0,1:T(4,128)S(1)} %fusion.36), kind=kOutput, calls=%fused_computation.51 | convolution fusion | flops 404783104 | bytes 139264 | tf_op jit(solution)/shard_map/ckr,rd->ckd/dot_general | solution.py:90
  49.3 3.5 %all-to-all-start = ((s32[16,1,256]{2,1,0:T(1,128)}), s32[16,1,256]{2,1,0:T(1,128)S(1)}, u32[]{:S(2)}, u32[]{:S(2)}) async-start(s32[16,1,256]{2,1,0:T(1,128)} %reshape.345), calls=%async_computation | async-start | bytes 32768 | tf_op jit(solution)/shard_map/all_to_all | solution.py:109
  53.7 5.5 %all-to-all-done = s32[16,1,256]{2,1,0:T(1,128)S(1)} async-done(((s32[16,1,256]{2,1,0:T(1,128)}), s32[16,1,256]{2,1,0:T(1,128)S(1)}, u32[]{:S(2)}, u32[]{:S(2)}) %all-to-all-start) | async-done | bytes 16416 | tf_op jit(solution)/shard_map/all_to_all | solution.py:109
  59.2 3.5 %all-to-all-start.2 = ((f32[16,1,768]{2,1,0:T(1,128)}), f32[16,1,768]{2,1,0:T(1,128)S(1)}, u32[]{:S(2)}, u32[]{:S(2)}) async-start(f32[16,1,768]{2,1,0:T(1,128)} %reshape.347), calls=%async_computation.2 | async-start | bytes 98304 | tf_op jit(solution)/shard_map/all_to_all | solution.py:102
  64.7 4.5 %all-to-all-done.2 = f32[16,1,768]{2,1,0:T(1,128)S(1)} async-done(((f32[16,1,768]{2,1,0:T(1,128)}), f32[16,1,768]{2,1,0:T(1,128)S(1)}, u32[]{:S(2)}, u32[]{:S(2)}) %all-to-all-start.2) | async-done | bytes 49184 | tf_op jit(solution)/shard_map/all_to_all | solution.py:102
  69.2 24.4 %all-to-all-start.1 = ((s32[1,4,16,64]{2,1,0,3:T(4,128)}), s32[1,4,16,64]{2,1,0,3:T(4,128)S(1)}, u32[]{:S(2)}, u32[]{:S(2)}) async-start(s32[1,4,16,64]{2,1,0,3:T(4,128)} %copy.15), calls=%async_computation.1 | async-start | bytes 262144 | tf_op jit(solution)/shard_map/all_to_all | solution.py:108
  95.3 0.9 reshape.349
  96.2 28.1 %all-to-all-done.1 = s32[1,4,16,64]{2,1,0,3:T(4,128)S(1)} async-done(((s32[1,4,16,64]{2,1,0,3:T(4,128)}), s32[1,4,16,64]{2,1,0,3:T(4,128)S(1)}, u32[]{:S(2)}, u32[]{:S(2)}) %all-to-all-start.1) | async-done | bytes 16416 | tf_op jit(solution)/shard_map/all_to_all | solution.py:108
  124.3 5.4 %all-to-all-start.3 = ((f32[64,1,192]{2,1,0:T(1,128)}), f32[64,1,192]{2,1,0:T(1,128)S(1)}, u32[]{:S(2)}, u32[]{:S(2)}) async-start(f32[64,1,192]{2,1,0:T(1,128)} %reshape.349), calls=%async_computation.3 | async-start | bytes 131072 | tf_op jit(solution)/shard_map/all_to_all | solution.py:101
  130.0 25.1 %all-to-all-done.3 = f32[64,1,192]{2,1,0:T(1,128)S(1)} async-done(((f32[64,1,192]{2,1,0:T(1,128)}), f32[64,1,192]{2,1,0:T(1,128)S(1)}, u32[]{:S(2)}, u32[]{:S(2)}) %all-to-all-start.3) | async-done | bytes 49184 | tf_op jit(solution)/shard_map/all_to_all | solution.py:101
  156.4 1.0 fusion.21
  (113 shorter events, 16.3 us)
Async XLA Ops:
  0.8 16.3 %collective-permute-start = (f32[1,16,512]{2,1,0:T(8,128)S(1)}, f32[1,16,512]{2,1,0:T(8,128)S(1)}, u32[]{:S(2)}, u32[]{:S(2)}) collective-permute-start(f32[1,16,512]{2,1,0:T(8,128)S(1)} %slice.94), channel_id=1, source_target_pairs={{64,0},{128,64},{192,128},{256,192},{320,256},{384,320},{448,384},... | collective-permute-start | bytes 98312 | tf_op jit(solution)/shard_map/ppermute | solution.py:10
  12.1 4.9 %copy-start.1 = (s32[3,2048]{1,0:T(4,128)S(1)}, s32[3,2048]{1,0:T(4,128)}, u32[]{:S(2)}) copy-start(s32[3,2048]{1,0:T(4,128)} %param.8) | copy-start | bytes 73732
  12.1 4.9 %copy-start = (f32[16,16,512]{2,1,0:T(8,128)S(1)}, f32[16,16,512]{2,1,0:T(8,128)}, u32[]{:S(2)}) copy-start(f32[16,16,512]{2,1,0:T(8,128)} %param.7) | copy-start | bytes 1572868
  17.1 9.3 %collective-permute-start.1 = (f32[17,1,512]{2,1,0:T(1,128)S(1)}, f32[17,1,512]{2,1,0:T(1,128)S(1)}, u32[]{:S(2)}, u32[]{:S(2)}) collective-permute-start(f32[17,1,512]{2,1,0:T(1,128)S(1)} %slice.101), channel_id=1, source_target_pairs={{1,0},{2,1},{3,2},{4,3},{5,4},{6,5},{7,6},{8,7},{9,8},{10,9},{11,1... | collective-permute-start | bytes 104456 | tf_op jit(solution)/shard_map/ppermute | solution.py:10
  26.6 18.9 %copy-start.2 = (s32[2048,1]{0,1:T(1,128)S(1)}, s32[2048,1]{0,1:T(1,128)}, u32[]{:S(2)}) copy-start(s32[2048,1]{0,1:T(1,128)} %param.10) | copy-start | bytes 24580
  49.3 9.9 %all-to-all-start = ((s32[16,1,256]{2,1,0:T(1,128)}), s32[16,1,256]{2,1,0:T(1,128)S(1)}, u32[]{:S(2)}, u32[]{:S(2)}) async-start(s32[16,1,256]{2,1,0:T(1,128)} %reshape.345), calls=%async_computation | async-start | bytes 32768 | tf_op jit(solution)/shard_map/all_to_all | solution.py:109
  59.2 10.0 %all-to-all-start.2 = ((f32[16,1,768]{2,1,0:T(1,128)}), f32[16,1,768]{2,1,0:T(1,128)S(1)}, u32[]{:S(2)}, u32[]{:S(2)}) async-start(f32[16,1,768]{2,1,0:T(1,128)} %reshape.347), calls=%async_computation.2 | async-start | bytes 98304 | tf_op jit(solution)/shard_map/all_to_all | solution.py:102
  69.2 55.1 %all-to-all-start.1 = ((s32[1,4,16,64]{2,1,0,3:T(4,128)}), s32[1,4,16,64]{2,1,0,3:T(4,128)S(1)}, u32[]{:S(2)}, u32[]{:S(2)}) async-start(s32[1,4,16,64]{2,1,0,3:T(4,128)} %copy.15), calls=%async_computation.1 | async-start | bytes 262144 | tf_op jit(solution)/shard_map/all_to_all | solution.py:108
  124.3 30.8 %all-to-all-start.3 = ((f32[64,1,192]{2,1,0:T(1,128)}), f32[64,1,192]{2,1,0:T(1,128)S(1)}, u32[]{:S(2)}, u32[]{:S(2)}) async-start(f32[64,1,192]{2,1,0:T(1,128)} %reshape.349), calls=%async_computation.3 | async-start | bytes 131072 | tf_op jit(solution)/shard_map/all_to_all | solution.py:101
where the time goes:
time: 159 us; the launch traced here: 158 us
  waiting for transfers between devices  64.1 us (40%)
  starting transfers between devices  52.9 us (33%)
  matrix products  17.7 us (11%)
  local copies, waits for them, and re-layouts  11.9 us (7%)
  other arithmetic  10.7 us (7%)
    all_to_all x1, waiting for transfers between devices, body(): lax.all_to_all(lax.all_to_all(send_slot, 'gz', split_axis=2, concat_axis=...  28.1 us
    all_to_all x1, waiting for transfers between devices, body(): lax.all_to_all(lax.all_to_all(send_grad, 'gz', split_axis=2, concat_axis=...  25.1 us
    all_to_all x1, starting transfers between devices, body(): lax.all_to_all(lax.all_to_all(send_slot, 'gz', split_axis=2, concat_axis=...  24.4 us
    ppermute x2, starting transfers between devices, from_behind(): return lax.ppermute(block, axis, route)  16 us
    dot_general x4, matrix products, read_block(): lax.dot_general(stacked, plane, (((1,), (1,)), ((), ())), precision=lax.P...  8.93 us
    all_to_all x1, waiting for transfers between devices, body(): lax.all_to_all(send_slot, 'gz', split_axis=2, concat_axis=2, tiled=True)  5.49 us
    all_to_all x1, starting transfers between devices, body(): lax.all_to_all(lax.all_to_all(send_grad, 'gz', split_axis=2, concat_axis=...  5.41 us
    dot_general x1, matrix products, body(): jnp.einsum('ij,gjd->gid', lower_tri, grouped, preferred_element_type=jnp....  4.84 us
  transfers between devices with their start and end apart: 6, of which 5 were waited for; matrix products, arithmetic and copies ran while one was open for 9% of the time, Pallas kernels for 0%

commit v1 on v0

v1 whole, which is shorter than its diff:
```python
import jax
import jax.numpy as jnp
from jax import lax
from jax.experimental import pallas as pl
from jax.experimental.pallas import tpu as pltpu
from jax.sharding import Mesh, PartitionSpec as P

F32 = jnp.float32
BF16 = jnp.bfloat16
TILE = 256


def split(x):
    high = x.astype(BF16)
    return high, (x - high.astype(F32)).astype(BF16)


def hot(mask):
    return jnp.where(mask, 1.0, 0.0).astype(BF16)


def rows_of(shape):
    return lax.broadcasted_iota(jnp.int32, shape, 0)


def lane_tile(ref, row, t):
    return ref[row : row + 1, t * TILE : (t + 1) * TILE]


def fraction_of(offsets):
    return (offsets.astype(F32) + 0.5) / 1024.0


def two_weights(index, frac, place):
    lower = place == index
    upper = place == index + 1
    weight = jnp.where(lower, 1.0 - frac, jnp.where(upper, frac, 0.0))
    slope = jnp.where(upper, 1.0, jnp.where(lower, -1.0, 0.0))
    return weight, slope


def with_next_x(block):
    return block, pltpu.roll(block, block.shape[1] - 1, 1) - block


def count_earlier(owner_row):
    num_rows = owner_row.shape[1]
    chunks = num_rows // 128
    names = owner_row.astype(F32)
    columns = jnp.concatenate([names[:, i * 128 : (i + 1) * 128] for i in range(chunks)], 0)
    columns = jnp.concatenate([columns, jnp.zeros((128 - chunks, 128), F32)], 0).T
    earlier = rows_of((128, 128)) < lax.broadcasted_iota(jnp.int32, (128, 128), 1)
    counts = [jnp.zeros((8, 128), F32)] * chunks
    for i in range(chunks):
        column = jnp.broadcast_to(columns[:, i : i + 1], (128, 128))
        for j in range(i, chunks):
            same = column == names[:, j * 128 : (j + 1) * 128]
            if i == j:
                same = same & earlier
            ones = jnp.where(same, 1.0, 0.0)
            counts[j] = counts[j] + jnp.sum(ones.reshape(16, 8, 128), axis=0)
    return jnp.concatenate([jnp.sum(c, axis=0, keepdims=True) for c in counts], 1)


def inner_kernel(grid_ref, cells_ref, offsets_ref, owners_ref, grad_ref, place_ref, lhs_ref):
    rows, size_x = grid_ref.shape
    for part, block in enumerate(with_next_x(grid_ref[...])):
        for half, piece in enumerate(split(block)):
            lhs_ref[part * rows : (part + 1) * rows, half * size_x : (half + 1) * size_x] = piece
    owners = owners_ref[...]
    rank = count_earlier(owners).astype(jnp.int32)
    place_ref[...] = ((owners >> 6) * 2 + (owners & 1)) * 4 + rank
    for t in range(cells_ref.shape[1] // TILE):
        at_x = hot(rows_of((size_x, TILE)) == lane_tile(cells_ref, 2, t))
        read = jnp.dot(lhs_ref[...], jnp.concatenate([at_x, at_x], 0), preferred_element_type=F32)
        frac = [fraction_of(lane_tile(offsets_ref, a, t)) for a in range(3)]
        index_z = lane_tile(cells_ref, 0, t) & 15
        index_y = lane_tile(cells_ref, 1, t) & 15
        sum_z = sum_y = sum_x = jnp.zeros((16, TILE), F32)
        for z in range(16):
            diff = read[rows + z * 16 : rows + (z + 1) * 16]
            value = read[z * 16 : (z + 1) * 16] + diff * frac[2]
            weight_z, slope_z = two_weights(index_z, frac[0], z)
            sum_z = sum_z + value * slope_z
            sum_y = sum_y + value * weight_z
            sum_x = sum_x + diff * weight_z
        weight_y, slope_y = two_weights(index_y, frac[1], rows_of((16, TILE)))
        parts = [sum_z * weight_y, sum_y * slope_y, sum_x * weight_y]
        sums = [jnp.sum(p, axis=0, keepdims=True) for p in parts]
        grad_ref[:, t * TILE : (t + 1) * TILE] = jnp.concatenate(
            sums + [jnp.zeros((5, TILE), F32)], 0
        )


def send_kernel(
    face_z_ref, face_y_ref, edge_ref, grad_ref, place_ref, cells_ref, offsets_ref, owners_ref,
    slots_ref, send_ref, halo_ref, value_ref, hot_ref,
):
    size_x = edge_ref.shape[1]
    edge = jnp.broadcast_to(edge_ref[...], (8, size_x))
    halo = jnp.concatenate([face_z_ref[...], face_y_ref[...], edge], 0)
    count = halo.shape[0]
    for part, block in enumerate(with_next_x(halo)):
        for half, piece in enumerate(split(block)):
            halo_ref[(2 * half + part) * count : (2 * half + part + 1) * count, :] = piece
    for t in range(cells_ref.shape[1] // TILE):
        lanes = slice(t * TILE, (t + 1) * TILE)
        at_x = hot(rows_of((size_x, TILE)) == lane_tile(cells_ref, 2, t))
        read = jnp.dot(halo_ref[...], at_x, preferred_element_type=F32)
        read = read[: 2 * count] + read[2 * count :]
        frac = [fraction_of(lane_tile(offsets_ref, a, t)) for a in range(3)]
        index_z = lane_tile(cells_ref, 0, t) & 15
        index_y = lane_tile(cells_ref, 1, t) & 15
        diff = read[count:]
        value = read[:count] + diff * frac[2]
        weight_z, slope_z = two_weights(index_z, frac[0], rows_of((16, TILE)))
        weight_y, slope_y = two_weights(index_y, frac[1], rows_of((16, TILE)))
        top_z, step_z = two_weights(index_z, frac[0], 16)
        top_y, step_y = two_weights(index_y, frac[1], 16)

        def over(block, weight):
            return jnp.sum(block * weight, axis=0, keepdims=True)

        on_z, on_y, on_edge = value[:16], value[16:32], value[32:33]
        dif_z, dif_y, dif_edge = diff[:16], diff[16:32], diff[32:33]
        grad_z = step_z * (over(on_z, weight_y) + top_y * on_edge) + top_y * over(on_y, slope_z)
        grad_y = top_z * (over(on_z, slope_y) + step_y * on_edge) + step_y * over(on_y, weight_z)
        grad_x = top_z * (over(dif_z, weight_y) + top_y * dif_edge) + top_y * over(dif_y, weight_z)
        grad_z = grad_z + grad_ref[0:1, lanes]
        grad_y = grad_y + grad_ref[1:2, lanes]
        grad_x = grad_x + grad_ref[2:3, lanes]
        slot = slots_ref[:, lanes].astype(F32)
        kind = rows_of((8, TILE)) & 3
        four = jnp.where(
            kind == 0, grad_z, jnp.where(kind == 1, grad_y, jnp.where(kind == 2, grad_x, slot))
        )
        owner_z = (owners_ref[:, lanes] >> 1) & 31
        here = (rows_of((128, TILE)) >> 2) == owner_z
        for half, piece in enumerate(split(four)):
            tall = jnp.concatenate([piece.astype(F32)] * 16, 0)
            value_ref[half * 128 : (half + 1) * 128, lanes] = jnp.where(here, tall, 0.0).astype(BF16)
        hot_ref[:, lanes] = hot(rows_of((128, TILE)) == place_ref[:, lanes])
    both = lax.dot_general(
        value_ref[...], hot_ref[...], (((1,), (1,)), ((), ())), preferred_element_type=F32
    )
    send_ref[...] = both[:128] + both[128:]


def turn_kernel(in_ref, out_ref):
    out_ref[...] = in_ref[...].T


def place_kernel(recv_ref, out_ref, value_ref, hot_ref):
    turned = recv_ref[...].T
    high, low = split(turned)
    halves = (high.astype(F32), low.astype(F32))
    for j in range(32):
        lanes = slice(j * 128, (j + 1) * 128)
        slot = turned[4 * j + 3 : 4 * j + 4].astype(jnp.int32)
        here = (rows_of((64, 128)) >> 2) == (slot >> 7)
        for half, piece in enumerate(halves):
            four = piece[4 * j : 4 * j + 4]
            eight = jnp.concatenate([four, four], 0)
            tall = jnp.concatenate([eight] * 8, 0)
            value_ref[half * 64 : (half + 1) * 64, lanes] = jnp.where(here, tall, 0.0).astype(BF16)
        hot_ref[:, lanes] = hot(rows_of((128, 128)) == (slot & 127))
    both = lax.dot_general(
        value_ref[...], hot_ref[...], (((1,), (1,)), ((), ())), preferred_element_type=F32
    )
    total = both[:64] + both[64:]
    for h in range(16):
        out_ref[:, h * 128 : (h + 1) * 128] = total[4 * h : 4 * h + 3]


def run_inner(plane, cells, offsets, owner_row):
    rows, size_x = plane.shape
    num_rows = cells.shape[1]
    return pl.pallas_call(
        inner_kernel,
        out_shape=(
            jax.ShapeDtypeStruct((8, num_rows), F32),
            jax.ShapeDtypeStruct((1, num_rows), jnp.int32),
        ),
        scratch_shapes=[pltpu.VMEM((2 * rows, 2 * size_x), BF16)],
        cost_estimate=pl.CostEstimate(
            flops=8 * rows * size_x * num_rows, bytes_accessed=1000000, transcendentals=0
        ),
        name="inner",
    )(plane, cells, offsets, owner_row)


def run_send(face_z, face_y, edge, grad, place, cells, offsets, owner_row, slot_row):
    num_rows = cells.shape[1]
    return pl.pallas_call(
        send_kernel,
        out_shape=jax.ShapeDtypeStruct((128, 128), F32),
        scratch_shapes=[
            pltpu.VMEM((160, edge.shape[1]), BF16),
            pltpu.VMEM((256, num_rows), BF16),
            pltpu.VMEM((128, num_rows), BF16),
        ],
        name="send",
    )(face_z, face_y, edge, grad, place, cells, offsets, owner_row, slot_row)


def run_turn(x):
    return pl.pallas_call(
        turn_kernel, out_shape=jax.ShapeDtypeStruct((128, 128), F32), name="turn"
    )(x)


def run_place(received, num_rows):
    return pl.pallas_call(
        place_kernel,
        out_shape=jax.ShapeDtypeStruct((3, num_rows), F32),
        scratch_shapes=[pltpu.VMEM((128, 4096), BF16), pltpu.VMEM((128, 4096), BF16)],
        name="place",
    )(received)


def body(grid_grad, cells, offsets, owners, slots):
    block_z, block_y, size_x = grid_grad.shape
    num_rows = cells.shape[1]
    count_z = lax.axis_size("gz")
    count_y = lax.axis_size("z") * lax.axis_size("c")
    next_z = [((i + 1) % count_z, i) for i in range(count_z)]
    next_y = [((i + 1) % count_y, i) for i in range(count_y)]
    next_zy = [
        (sz * count_y + sy, dz * count_y + dy) for sz, dz in next_z for sy, dy in next_y
    ]
    face_z = lax.ppermute(grid_grad[0], "gz", next_z)
    face_y = lax.ppermute(grid_grad[:, 0], ("z", "c"), next_y)
    edge = lax.ppermute(grid_grad[0, :1], ("gz", "z", "c"), next_zy)
    owner_row = owners.reshape(1, num_rows)
    slot_row = slots.reshape(1, num_rows)
    plane = grid_grad.reshape(block_z * block_y, size_x)
    grad, place = run_inner(plane, cells, offsets, owner_row)
    send = run_send(face_z, face_y, edge, grad, place, cells, offsets, owner_row, slot_row)
    along_z = lax.all_to_all(send, "z", 0, 0, tiled=True)
    received = lax.all_to_all(run_turn(along_z), ("gz", "c"), 0, 0, tiled=True)
    return run_place(received, num_rows)


def solution(mesh):
    fine = Mesh(mesh.devices.reshape(16, 32, 2), ("gz", "z", "c"))
    every = ("gz", "z", "c")
    placed = (P("gz", ("z", "c"), None), P(None, every), P(None, every), P(every, None), P(every))
    return jax.shard_map(
        body, mesh=fine, in_specs=placed, out_specs=P(None, every), check_vma=False
    )
```

time: 159 us -> 93.4 us (0.59)
  waiting for transfers between devices: 64.1 us -> 0.01 us
  blocking collectives: 0 us -> 50.8 us
  starting transfers between devices: 52.9 us -> 26.9 us
  matrix products: 17.7 us -> 0 us
  Pallas kernels: 0 us -> 12.1 us
  other arithmetic: 10.7 us -> 0 us
  local copies, waits for them, and re-layouts: 11.9 us -> 3.06 us
    all_to_all x4 -> x0, waiting for transfers between devices: 63.2 us -> none  [the longest x1 28.1 us: body(): lax.all_to_all(lax.all_to_all(send_slot, 'gz', split_axis=2, concat_axis=...]
    all_to_all x0 -> x2, blocking collectives: none -> 50.8 us  [the longest x1 36.5 us: body(): along_z = lax.all_to_all(send, 'z', 0, 0, tiled=True)]
    all_to_all x4 -> x0, starting transfers between devices: 36.8 us -> none  [the longest x1 24.4 us: body(): lax.all_to_all(lax.all_to_all(send_slot, 'gz', split_axis=2, concat_axis=...]
    dot_general x7 -> x0, matrix products: 17.7 us -> none  [the longest x4 8.93 us: read_block(): lax.dot_general(stacked, plane, (((1,), (1,)), ((), ())), precision=lax.P...]
    pallas_call x0 -> x4, Pallas kernels: none -> 12.1 us  [the longest x1 5.38 us: run_inner(): pl.pallas_call(inner_kernel, out_shape=(jax.ShapeDtypeStruct((8, num_rows...]
    ppermute x2 -> x3, starting transfers between devices: 16 us -> 26.9 us  [the longest x1 16.3 us: body(): face_y = lax.ppermute(grid_grad[:, 0], ('z', 'c'), next_y)]
    reduce_sum x13 -> x0, other arithmetic: 4.82 us -> none  [the longest x1 2.06 us: body(): group_counts = jnp.sum(grouped.astype(jnp.float32), axis=1)]
    reshape x9 -> x0, local copies, waits for them, and re-layouts: 4.46 us -> none  [the longest x4 4.02 us: read_block(): projected = projected.reshape(2, index.shape[1], ext_z, ext_y)]
  transfers between devices with their start and end apart: 6 -> 3, of which waited for: 5 -> 0; matrix products, arithmetic and copies ran while one was open for 9% -> 2% of each run, Pallas kernels for 0% -> 6%
where the time goes in v1:
time: 93.4 us; the launch traced here: 92.8 us
  blocking collectives  50.8 us (54%)
  starting transfers between devices  26.9 us (29%)
  Pallas kernels  12.1 us (13%)
  local copies, waits for them, and re-layouts  3.06 us (3%)
    all_to_all x1, blocking collectives, body(): along_z = lax.all_to_all(send, 'z', 0, 0, tiled=True)  36.5 us
    ppermute x1, starting transfers between devices, body(): face_y = lax.ppermute(grid_grad[:, 0], ('z', 'c'), next_y)  16.3 us
    all_to_all x1, blocking collectives, body(): received = lax.all_to_all(run_turn(along_z), ('gz', 'c'), 0, 0, tiled=True)  14.2 us
    ppermute x1, starting transfers between devices, body(): edge = lax.ppermute(grid_grad[0, :1], ('gz', 'z', 'c'), next_zy)  8.2 us
    pallas_call x1, Pallas kernels, run_inner(): pl.pallas_call(inner_kernel, out_shape=(jax.ShapeDtypeStruct((8, num_rows...  5.38 us
    pallas_call x1, Pallas kernels, run_send(): pl.pallas_call(send_kernel, out_shape=jax.ShapeDtypeStruct((128, 128), F3...  2.72 us
    pallas_call x1, Pallas kernels, run_place(): pl.pallas_call(place_kernel, out_shape=jax.ShapeDtypeStruct((3, num_rows)...  2.4 us
    ppermute x1, starting transfers between devices, body(): face_z = lax.ppermute(grid_grad[0], 'gz', next_z)  2.36 us
  transfers between devices with their start and end apart: 3, of which 0 were waited for; matrix products, arithmetic and copies ran while one was open for 2% of the time, Pallas kernels for 6%

profile of v1, /device:TPU:1, one launch (start us, length us, event | category | flops | bytes accessed | tf_op | source)
XLA Modules:
  0.0 92.8 jit_solution(6119748197024926959)
XLA Ops:
  0.0 0.7 slice_bitcast_fusion.1
  0.7 8.2 %collective-permute-start.2 = (f32[1,512]{1,0:T(1,128)S(1)}, f32[1,512]{1,0:T(1,128)S(1)}, u32[]{:S(2)}, u32[]{:S(2)}) collective-permute-start(f32[1,512]{1,0:T(1,128)S(1)} %slice_bitcast_fusion.1), channel_id=1, source_target_pairs={{65,0},{66,1},{67,2},{68,3},{69,4},{70,5},{71,6},{72,7},{73,8},{74... | collective-permute-start | bytes 6152 | tf_op jit(solution)/shard_map/ppermute | solution.py:233
  8.9 0.8 slice_bitcast_fusion
  9.7 2.4 %collective-permute-start = (f32[16,512]{1,0:T(8,128)S(1)}, f32[16,512]{1,0:T(8,128)S(1)}, u32[]{:S(2)}, u32[]{:S(2)}) collective-permute-start(f32[16,512]{1,0:T(8,128)S(1)} %slice_bitcast_fusion), channel_id=1, source_target_pairs={{64,0},{128,64},{192,128},{256,192},{320,256},{384,320},{448,384},... | collective-permute-start | bytes 98312 | tf_op jit(solution)/shard_map/ppermute | solution.py:231
  12.1 1.0 %slice.10 = f32[16,1,512]{2,1,0:T(1,128)S(1)} slice(f32[16,16,512]{2,1,0:T(8,128)} %param.5), slice={[0:16], [0:1], [0:512]} | slice | bytes 65536 | tf_op jit(solution)/shard_map/slice | solution.py:232
  13.0 16.3 %collective-permute-start.1 = (f32[16,512]{1,0:T(8,128)S(1)}, f32[16,512]{1,0:T(8,128)S(1)}, u32[]{:S(2)}, u32[]{:S(2)}) collective-permute-start(f32[16,512]{1,0:T(8,128)S(1)} %bitcast.18), channel_id=1, source_target_pairs={{1,0},{2,1},{3,2},{4,3},{5,4},{6,5},{7,6},{8,7},{9,8},{10,9},{11,1... | collective-permute-start | bytes 98312 | tf_op jit(solution)/shard_map/ppermute | solution.py:232
  29.4 5.4 %inner.1 = (f32[8,2048]{1,0:T(8,128)}, s32[1,2048]{1,0:T(1,128)}) custom-call(f32[256,512]{1,0:T(8,128)} %bitcast.19, s32[3,2048]{1,0:T(4,128)} %cells_ref.3, s32[3,2048]{1,0:T(4,128)} %offsets_ref.3, s32[1,2048]{1,0:T(1,128)} %bitcast.20), custom_call_target="tpu_custom_call" | custom-call | flops 2147483648 | bytes 1000000 | tf_op jit(solution)/shard_map/inner/pallas_call | solution.py:178
  34.8 0.0 collective-permute-done.2.edge_ref
  34.8 0.0 copy-start.2
  34.8 0.0 collective-permute-done.face_z_ref
  34.8 0.0 copy-start
  34.8 0.0 collective-permute-done.1.face_y_ref
  34.8 0.0 copy-start.1
  34.8 0.6 copy-done.2
  35.4 0.0 copy-done
  35.4 0.0 copy-done.1
  35.4 2.7 %send.1 = f32[128,128]{1,0:T(8,128)} custom-call(f32[16,512]{1,0:T(8,128)} %copy-done, f32[16,512]{1,0:T(8,128)} %copy-done.1, f32[1,512]{1,0:T(1,128)} %copy-done.2, f32[8,2048]{1,0:T(8,128)} %get-tuple-element.7.grad_ref, s32[1,2048]{1,0:T(1,128)} %get-tuple-element.8.place_ref, s32[3,2048]{1,0:T(4,128)} %cells_ref.3, s32[3,2048]{1,0:T(4,128)} %offsets_ref.3, ...), custom_call_target="tpu_custom_call" | custom-call | tf_op jit(solution)/shard_map/send/pallas_call | solution.py:194
  38.1 36.5 %all_to_all.22 = f32[32,4,128]{2,1,0:T(4,128)} all-to-all(f32[32,4,128]{2,1,0:T(4,128)} %bitcast.17), channel_id=1, replica_groups=mesh['gz'=16,'z'=32,'c'=2] {'z'}, dimensions={0} | all-to-all | bytes 131072 | tf_op jit(solution)/shard_map/all_to_all | solution.py:239
  74.7 1.6 %turn.1 = f32[128,128]{1,0:T(8,128)} custom-call(f32[128,128]{1,0:T(8,128)} %bitcast.14), custom_call_target="tpu_custom_call" | custom-call | tf_op jit(solution)/shard_map/turn/pallas_call | solution.py:207
  76.2 14.2 %all_to_all.23 = f32[32,4,128]{2,1,0:T(4,128)} all-to-all(f32[32,4,128]{2,1,0:T(4,128)} %bitcast.15), channel_id=1, replica_groups=mesh['gz'=16,'z'=32,'c'=2] {'gz','c'}, dimensions={0} | all-to-all | bytes 131072 | tf_op jit(solution)/shard_map/all_to_all | solution.py:240
  90.5 2.4 %place.1 = f32[3,2048]{1,0:T(4,128)} custom-call(f32[128,128]{1,0:T(8,128)} %bitcast.16), custom_call_target="tpu_custom_call" | custom-call | tf_op jit(solution)/shard_map/place/pallas_call | solution.py:213
  (1 shorter events, 0.0 us)
Async XLA Ops:
  0.7 34.0 %collective-permute-start.2 = (f32[1,512]{1,0:T(1,128)S(1)}, f32[1,512]{1,0:T(1,128)S(1)}, u32[]{:S(2)}, u32[]{:S(2)}) collective-permute-start(f32[1,512]{1,0:T(1,128)S(1)} %slice_bitcast_fusion.1), channel_id=1, source_target_pairs={{65,0},{66,1},{67,2},{68,3},{69,4},{70,5},{71,6},{72,7},{73,8},{74... | collective-permute-start | bytes 6152 | tf_op jit(solution)/shard_map/ppermute | solution.py:233
  9.7 25.1 %collective-permute-start = (f32[16,512]{1,0:T(8,128)S(1)}, f32[16,512]{1,0:T(8,128)S(1)}, u32[]{:S(2)}, u32[]{:S(2)}) collective-permute-start(f32[16,512]{1,0:T(8,128)S(1)} %slice_bitcast_fusion), channel_id=1, source_target_pairs={{64,0},{128,64},{192,128},{256,192},{320,256},{384,320},{448,384},... | collective-permute-start | bytes 98312 | tf_op jit(solution)/shard_map/ppermute | solution.py:231
  13.0 21.7 %collective-permute-start.1 = (f32[16,512]{1,0:T(8,128)S(1)}, f32[16,512]{1,0:T(8,128)S(1)}, u32[]{:S(2)}, u32[]{:S(2)}) collective-permute-start(f32[16,512]{1,0:T(8,128)S(1)} %bitcast.18), channel_id=1, source_target_pairs={{1,0},{2,1},{3,2},{4,3},{5,4},{6,5},{7,6},{8,7},{9,8},{10,9},{11,1... | collective-permute-start | bytes 98312 | tf_op jit(solution)/shard_map/ppermute | solution.py:232
  34.8 0.6 copy-start.2
  34.8 0.6 copy-start
  34.8 0.6 copy-start.1

commit v2 on v1

--- a/solution.py
+++ b/solution.py
@@ -8,6 +8,7 @@
 F32 = jnp.float32
 BF16 = jnp.bfloat16
 TILE = 256
+SMALL = pltpu.CompilerParams(vmem_limit_bytes=16 * 1024 * 1024)
 
 
 def split(x):
@@ -60,6 +61,14 @@
             ones = jnp.where(same, 1.0, 0.0)
             counts[j] = counts[j] + jnp.sum(ones.reshape(16, 8, 128), axis=0)
     return jnp.concatenate([jnp.sum(c, axis=0, keepdims=True) for c in counts], 1)
+
+
+def faces_kernel(grid_ref, face_z_ref, face_y_ref, edge_ref):
+    block_z, block_y = face_y_ref.shape[0], face_z_ref.shape[0]
+    face_z_ref[...] = grid_ref[:block_y]
+    edge_ref[...] = grid_ref[:1]
+    for z in range(block_z):
+        face_y_ref[z : z + 1] = grid_ref[z * block_y : z * block_y + 1]
 
 
 def inner_kernel(grid_ref, cells_ref, offsets_ref, owners_ref, grad_ref, place_ref, lhs_ref):
@@ -172,6 +181,20 @@
         out_ref[:, h * 128 : (h + 1) * 128] = total[4 * h : 4 * h + 3]
 
 
+def run_faces(plane, block_z, block_y):
+    size_x = plane.shape[1]
+    return pl.pallas_call(
+        faces_kernel,
+        out_shape=(
+            jax.ShapeDtypeStruct((block_y, size_x), F32),
+            jax.ShapeDtypeStruct((block_z, size_x), F32),
+            jax.ShapeDtypeStruct((1, size_x), F32),
+        ),
+        compiler_params=SMALL,
+        name="faces",
+    )(plane)
+
+
 def run_inner(plane, cells, offsets, owner_row):
     rows, size_x = plane.shape
     num_rows = cells.shape[1]
@@ -182,6 +205,7 @@
             jax.ShapeDtypeStruct((1, num_rows), jnp.int32),
         ),
         scratch_shapes=[pltpu.VMEM((2 * rows, 2 * size_x), BF16)],
+        compiler_params=SMALL,
         cost_estimate=pl.CostEstimate(
             flops=8 * rows * size_x * num_rows, bytes_accessed=1000000, transcendentals=0
         ),
@@ -199,13 +223,17 @@
             pltpu.VMEM((256, num_rows), BF16),
             pltpu.VMEM((128, num_rows), BF16),
         ],
+        compiler_params=SMALL,
         name="send",
     )(face_z, face_y, edge, grad, place, cells, offsets, owner_row, slot_row)
 
 
 def run_turn(x):
     return pl.pallas_call(
-        turn_kernel, out_shape=jax.ShapeDtypeStruct((128, 128), F32), name="turn"
+        turn_kernel,
+        out_shape=jax.ShapeDtypeStruct((128, 128), F32),
+        compiler_params=SMALL,
+        name="turn",
     )(x)
 
 
@@ -214,6 +242,7 @@
         place_kernel,
         out_shape=jax.ShapeDtypeStruct((3, num_rows), F32),
         scratch_shapes=[pltpu.VMEM((128, 4096), BF16), pltpu.VMEM((128, 4096), BF16)],
+        compiler_params=SMALL,
         name="place",
     )(received)
 
@@ -228,12 +257,13 @@
     next_zy = [
         (sz * count_y + sy, dz * count_y + dy) for sz, dz in next_z for sy, dy in next_y
     ]
-    face_z = lax.ppermute(grid_grad[0], "gz", next_z)
-    face_y = lax.ppermute(grid_grad[:, 0], ("z", "c"), next_y)
-    edge = lax.ppermute(grid_grad[0, :1], ("gz", "z", "c"), next_zy)
+    plane = grid_grad.reshape(block_z * block_y, size_x)
+    face_z, face_y, edge = run_faces(plane, block_z, block_y)
+    face_z = lax.ppermute(face_z, "gz", next_z)
+    face_y = lax.ppermute(face_y, ("z", "c"), next_y)
+    edge = lax.ppermute(edge, ("gz", "z", "c"), next_zy)
     owner_row = owners.reshape(1, num_rows)
     slot_row = slots.reshape(1, num_rows)
-    plane = grid_grad.reshape(block_z * block_y, size_x)
     grad, place = run_inner(plane, cells, offsets, owner_row)
     send = run_send(face_z, face_y, edge, grad, place, cells, offsets, owner_row, slot_row)
     along_z = lax.all_to_all(send, "z", 0, 0, tiled=True)

time: 93.4 us -> 85.5 us (0.915)
  Pallas kernels: 12.1 us -> 6.63 us
  local copies, waits for them, and re-layouts: 3.06 us -> 1.06 us
    pallas_call x1, Pallas kernels: 5.38 us -> 3.76 us  [run_inner(): pl.pallas_call(inner_kernel, out_shape=(jax.ShapeDtypeStruct((8, num_rows...]
    pallas_call x1, Pallas kernels: 2.72 us -> 1.22 us  [run_send(): pl.pallas_call(send_kernel, out_shape=jax.ShapeDtypeStruct((128, 128), F3...]
    squeeze x2 -> x0, local copies, waits for them, and re-layouts: 1.48 us -> none  [the longest x1 0.76 us: body(): face_z = lax.ppermute(grid_grad[0], 'gz', next_z)]
    pallas_call x1, Pallas kernels: 1.57 us -> 0.09 us  [run_turn(): pl.pallas_call(turn_kernel, out_shape=jax.ShapeDtypeStruct((128, 128), F3...]
    slice x1 -> x0, local copies, waits for them, and re-layouts: 0.97 us -> none  [body(): face_y = lax.ppermute(grid_grad[:, 0], ('z', 'c'), next_y)]
  transfers between devices with their start and end apart: 3 -> 3, of which waited for: 0 -> 0; matrix products, arithmetic and copies ran while one was open for 2% -> 0% of each run, Pallas kernels for 6% -> 4%
where the time goes in v2:
time: 85.5 us; the launch traced here: 85.2 us
  blocking collectives  50.3 us (59%)
  starting transfers between devices  27.1 us (32%)
  Pallas kernels  6.63 us (8%)
  local copies, waits for them, and re-layouts  1.06 us (1%)
    all_to_all x1, blocking collectives, body(): along_z = lax.all_to_all(send, 'z', 0, 0, tiled=True)  36.2 us
    ppermute x1, starting transfers between devices, body(): face_y = lax.ppermute(face_y, ('z', 'c'), next_y)  16.3 us
    all_to_all x1, blocking collectives, body(): received = lax.all_to_all(run_turn(along_z), ('gz', 'c'), 0, 0, tiled=True)  14.1 us
    ppermute x1, starting transfers between devices, body(): edge = lax.ppermute(edge, ('gz', 'z', 'c'), next_zy)  8.35 us
    pallas_call x1, Pallas kernels, run_inner(): pl.pallas_call(inner_kernel, out_shape=(jax.ShapeDtypeStruct((8, num_rows...  3.76 us
    ppermute x1, starting transfers between devices, body(): face_z = lax.ppermute(face_z, 'gz', next_z)  2.37 us
  transfers between devices with their start and end apart: 3, of which 0 were waited for; matrix products, arithmetic and copies ran while one was open for 0% of the time, Pallas kernels for 4%

profile of v2, /device:TPU:1, one launch (start us, length us, event | category | flops | bytes accessed | tf_op | source)
XLA Modules:
  0.0 85.2 jit_solution(43882420947153567)
XLA Ops:
  0.0 0.0 copy-start
  0.0 1.0 %copy-done = f32[16,16,512]{2,1,0:T(8,128)S(1)} copy-done((f32[16,16,512]{2,1,0:T(8,128)S(1)}, f32[16,16,512]{2,1,0:T(8,128)}, u32[]{:S(2)}) %copy-start) | copy-done | bytes 524312
  1.0 0.0 copy-start.1
  1.0 0.0 copy-start.2
  1.0 0.0 copy-start.3
  1.1 8.3 %collective-permute-start.2 = (f32[1,512]{1,0:T(1,128)S(1)}, f32[1,512]{1,0:T(1,128)S(1)}, u32[]{:S(2)}, u32[]{:S(2)}) collective-permute-start(f32[1,512]{1,0:T(1,128)S(1)} %get-tuple-element.12), channel_id=1, source_target_pairs={{65,0},{66,1},{67,2},{68,3},{69,4},{70,5},{71,6},{72,7},{73,8},{74... | collective-permute-start | bytes 6152 | tf_op jit(solution)/shard_map/ppermute | solution.py:264
  9.4 2.4 %collective-permute-start = (f32[16,512]{1,0:T(8,128)S(1)}, f32[16,512]{1,0:T(8,128)S(1)}, u32[]{:S(2)}, u32[]{:S(2)}) collective-permute-start(f32[16,512]{1,0:T(8,128)S(1)} %get-tuple-element.10), channel_id=1, source_target_pairs={{64,0},{128,64},{192,128},{256,192},{320,256},{384,320},{448,384},... | collective-permute-start | bytes 98312 | tf_op jit(solution)/shard_map/ppermute | solution.py:262
  11.8 16.3 %collective-permute-start.1 = (f32[16,512]{1,0:T(8,128)S(1)}, f32[16,512]{1,0:T(8,128)S(1)}, u32[]{:S(2)}, u32[]{:S(2)}) collective-permute-start(f32[16,512]{1,0:T(8,128)S(1)} %get-tuple-element.11), channel_id=1, source_target_pairs={{1,0},{2,1},{3,2},{4,3},{5,4},{6,5},{7,6},{8,7},{9,8},{10,9},{11,1... | collective-permute-start | bytes 98312 | tf_op jit(solution)/shard_map/ppermute | solution.py:263
  28.1 0.0 copy-done.1
  28.1 0.0 copy-done.2
  28.1 0.0 copy-done.3
  28.1 0.0 copy-start.4
  28.1 3.8 %inner.1 = (f32[8,2048]{1,0:T(8,128)S(1)}, s32[1,2048]{1,0:T(1,128)S(1)}) custom-call(f32[256,512]{1,0:T(8,128)S(1)} %bitcast.8, s32[3,2048]{1,0:T(4,128)S(1)} %copy-done.1, s32[3,2048]{1,0:T(4,128)S(1)} %copy-done.2, s32[1,2048]{1,0:T(1,128)S(1)} %bitcast.13), custom_call_target="tpu_custom_call" | custom-call | flops 2147483648 | bytes 1000000 | tf_op jit(solution)/shard_map/inner/pallas_call | solution.py:201
  31.9 0.0 collective-permute-done.2.edge_ref
  31.9 0.0 collective-permute-done.face_z_ref
  31.9 0.0 collective-permute-done.1.face_y_ref
  31.9 0.0 copy-done.4
  32.0 1.2 %send.1 = f32[128,128]{1,0:T(8,128)S(1)} custom-call(f32[16,512]{1,0:T(8,128)S(1)} %collective-permute-done.face_z_ref, f32[16,512]{1,0:T(8,128)S(1)} %collective-permute-done.1.face_y_ref, f32[1,512]{1,0:T(1,128)S(1)} %collective-permute-done.2.edge_ref, f32[8,2048]{1,0:T(8,128)S(1)} %get-tuple-element.13.grad_ref, ...), custom_call_target="tpu_custom_call" | custom-call | tf_op jit(solution)/shard_map/send/pallas_call | solution.py:218
  33.2 36.2 %all_to_all.22 = f32[32,4,128]{2,1,0:T(4,128)S(1)} all-to-all(f32[32,4,128]{2,1,0:T(4,128)S(1)} %bitcast.12), channel_id=1, replica_groups=mesh['gz'=16,'z'=32,'c'=2] {'z'}, dimensions={0} | all-to-all | bytes 131072 | tf_op jit(solution)/shard_map/all_to_all | solution.py:269
  69.4 0.1 turn.1
  69.5 14.1 %all_to_all.23 = f32[32,4,128]{2,1,0:T(4,128)S(1)} all-to-all(f32[32,4,128]{2,1,0:T(4,128)S(1)} %bitcast.10), channel_id=1, replica_groups=mesh['gz'=16,'z'=32,'c'=2] {'gz','c'}, dimensions={0} | all-to-all | bytes 131072 | tf_op jit(solution)/shard_map/all_to_all | solution.py:270
  83.6 1.6 %place.1 = f32[3,2048]{1,0:T(4,128)} custom-call(f32[128,128]{1,0:T(8,128)S(1)} %bitcast.11), custom_call_target="tpu_custom_call" | custom-call | tf_op jit(solution)/shard_map/place/pallas_call | solution.py:241
  (1 shorter events, 0.0 us)
Async XLA Ops:
  0.0 1.0 %copy-start = (f32[16,16,512]{2,1,0:T(8,128)S(1)}, f32[16,16,512]{2,1,0:T(8,128)}, u32[]{:S(2)}) copy-start(f32[16,16,512]{2,1,0:T(8,128)} %param.5) | copy-start | bytes 1572868
  1.0 27.1 %copy-start.1 = (s32[3,2048]{1,0:T(4,128)S(1)}, s32[3,2048]{1,0:T(4,128)}, u32[]{:S(2)}) copy-start(s32[3,2048]{1,0:T(4,128)} %cells_ref.3) | copy-start | bytes 73732
  1.0 27.1 %copy-start.2 = (s32[3,2048]{1,0:T(4,128)S(1)}, s32[3,2048]{1,0:T(4,128)}, u32[]{:S(2)}) copy-start(s32[3,2048]{1,0:T(4,128)} %offsets_ref.3) | copy-start | bytes 73732
  1.0 27.1 %copy-start.3 = (s32[2048,1]{0,1:T(1,128)S(1)}, s32[2048,1]{0,1:T(1,128)}, u32[]{:S(2)}) copy-start(s32[2048,1]{0,1:T(1,128)} %param.8) | copy-start | bytes 24580
  1.1 30.9 %collective-permute-start.2 = (f32[1,512]{1,0:T(1,128)S(1)}, f32[1,512]{1,0:T(1,128)S(1)}, u32[]{:S(2)}, u32[]{:S(2)}) collective-permute-start(f32[1,512]{1,0:T(1,128)S(1)} %get-tuple-element.12), channel_id=1, source_target_pairs={{65,0},{66,1},{67,2},{68,3},{69,4},{70,5},{71,6},{72,7},{73,8},{74... | collective-permute-start | bytes 6152 | tf_op jit(solution)/shard_map/ppermute | solution.py:264
  9.4 22.5 %collective-permute-start = (f32[16,512]{1,0:T(8,128)S(1)}, f32[16,512]{1,0:T(8,128)S(1)}, u32[]{:S(2)}, u32[]{:S(2)}) collective-permute-start(f32[16,512]{1,0:T(8,128)S(1)} %get-tuple-element.10), channel_id=1, source_target_pairs={{64,0},{128,64},{192,128},{256,192},{320,256},{384,320},{448,384},... | collective-permute-start | bytes 98312 | tf_op jit(solution)/shard_map/ppermute | solution.py:262
  11.8 20.1 %collective-permute-start.1 = (f32[16,512]{1,0:T(8,128)S(1)}, f32[16,512]{1,0:T(8,128)S(1)}, u32[]{:S(2)}, u32[]{:S(2)}) collective-permute-start(f32[16,512]{1,0:T(8,128)S(1)} %get-tuple-element.11), channel_id=1, source_target_pairs={{1,0},{2,1},{3,2},{4,3},{5,4},{6,5},{7,6},{8,7},{9,8},{10,9},{11,1... | collective-permute-start | bytes 98312 | tf_op jit(solution)/shard_map/ppermute | solution.py:263
  28.1 3.8 %copy-start.4 = (s32[2048]{0:T(1024)S(1)}, s32[2048]{0:T(1024)}, u32[]{:S(2)}) copy-start(s32[2048]{0:T(1024)} %param.9) | copy-start | bytes 24580

commit v3 on v2

--- a/solution.py
+++ b/solution.py
@@ -71,6 +71,38 @@
         face_y_ref[z : z + 1] = grid_ref[z * block_y : z * block_y + 1]
 
 
+def read_tiles(lhs_ref, cells_ref, offsets_ref, grad_ref):
+    rows, size_x = lhs_ref.shape[0] // 2, lhs_ref.shape[1] // 2
+    for t in range(cells_ref.shape[1] // TILE):
+        at_x = hot(rows_of((size_x, TILE)) == lane_tile(cells_ref, 2, t))
+        read = jnp.dot(lhs_ref[...], jnp.concatenate([at_x, at_x], 0), preferred_element_type=F32)
+        frac = [fraction_of(lane_tile(offsets_ref, a, t)) for a in range(3)]
+        index_z = jnp.broadcast_to(lane_tile(cells_ref, 0, t) & 15, (16, TILE))
+        index_y = lane_tile(cells_ref, 1, t) & 15
+        value = [jnp.zeros((16, TILE), F32)] * 2
+        diff = [jnp.zeros((16, TILE), F32)] * 2
+        for z in range(16):
+            value_z = read[z * 16 : (z + 1) * 16]
+            diff_z = read[rows + z * 16 : rows + (z + 1) * 16]
+            for side in range(2):
+                if z < side:
+                    continue
+                here = index_z == z - side
+                value[side] = jnp.where(here, value_z, value[side])
+                diff[side] = jnp.where(here, diff_z, diff[side])
+        low = value[0] + diff[0] * frac[2]
+        high = value[1] + diff[1] * frac[2]
+        weight_y, slope_y = two_weights(index_y, frac[1], rows_of((16, TILE)))
+        parts = [
+            (high - low) * weight_y,
+            (low * (1.0 - frac[0]) + high * frac[0]) * slope_y,
+            (diff[0] * (1.0 - frac[0]) + diff[1] * frac[0]) * weight_y,
+        ]
+        sums = [jnp.sum(p, axis=0, keepdims=True) for p in parts]
+        lanes = slice(t * TILE, (t + 1) * TILE)
+        grad_ref[:, lanes] = jnp.concatenate(sums + [jnp.zeros((5, TILE), F32)], 0)
+
+
 def inner_kernel(grid_ref, cells_ref, offsets_ref, owners_ref, grad_ref, place_ref, lhs_ref):
     rows, size_x = grid_ref.shape
     for part, block in enumerate(with_next_x(grid_ref[...])):
@@ -78,27 +110,8 @@
             lhs_ref[part * rows : (part + 1) * rows, half * size_x : (half + 1) * size_x] = piece
     owners = owners_ref[...]
     rank = count_earlier(owners).astype(jnp.int32)
-    place_ref[...] = ((owners >> 6) * 2 + (owners & 1)) * 4 + rank
-    for t in range(cells_ref.shape[1] // TILE):
-        at_x = hot(rows_of((size_x, TILE)) == lane_tile(cells_ref, 2, t))
-        read = jnp.dot(lhs_ref[...], jnp.concatenate([at_x, at_x], 0), preferred_element_type=F32)
-        frac = [fraction_of(lane_tile(offsets_ref, a, t)) for a in range(3)]
-        index_z = lane_tile(cells_ref, 0, t) & 15
-        index_y = lane_tile(cells_ref, 1, t) & 15
-        sum_z = sum_y = sum_x = jnp.zeros((16, TILE), F32)
-        for z in range(16):
-            diff = read[rows + z * 16 : rows + (z + 1) * 16]
-            value = read[z * 16 : (z + 1) * 16] + diff * frac[2]
-            weight_z, slope_z = two_weights(index_z, frac[0], z)
-            sum_z = sum_z + value * slope_z
-            sum_y = sum_y + value * weight_z
-            sum_x = sum_x + diff * weight_z
-        weight_y, slope_y = two_weights(index_y, frac[1], rows_of((16, TILE)))
-        parts = [sum_z * weight_y, sum_y * slope_y, sum_x * weight_y]
-        sums = [jnp.sum(p, axis=0, keepdims=True) for p in parts]
-        grad_ref[:, t * TILE : (t + 1) * TILE] = jnp.concatenate(
-            sums + [jnp.zeros((5, TILE), F32)], 0
-        )
+    place_ref[...] = ((owners >> 1) & 31) * 4 + rank
+    read_tiles(lhs_ref, cells_ref, offsets_ref, grad_ref)
 
 
 def send_kernel(
@@ -143,8 +156,8 @@
         four = jnp.where(
             kind == 0, grad_z, jnp.where(kind == 1, grad_y, jnp.where(kind == 2, grad_x, slot))
         )
-        owner_z = (owners_ref[:, lanes] >> 1) & 31
-        here = (rows_of((128, TILE)) >> 2) == owner_z
+        owners = owners_ref[:, lanes]
+        here = (rows_of((128, TILE)) >> 2) == (owners >> 6) * 2 + (owners & 1)
         for half, piece in enumerate(split(four)):
             tall = jnp.concatenate([piece.astype(F32)] * 16, 0)
             value_ref[half * 128 : (half + 1) * 128, lanes] = jnp.where(here, tall, 0.0).astype(BF16)
@@ -266,8 +279,8 @@
     slot_row = slots.reshape(1, num_rows)
     grad, place = run_inner(plane, cells, offsets, owner_row)
     send = run_send(face_z, face_y, edge, grad, place, cells, offsets, owner_row, slot_row)
-    along_z = lax.all_to_all(send, "z", 0, 0, tiled=True)
-    received = lax.all_to_all(run_turn(along_z), ("gz", "c"), 0, 0, tiled=True)
+    in_plane = lax.all_to_all(send, ("gz", "c"), 0, 0, tiled=True)
+    received = lax.all_to_all(run_turn(in_plane), "z", 0, 0, tiled=True)
     return run_place(received, num_rows)
 
 

time: 85.5 us -> 83.7 us (0.979)
  blocking collectives: 50.3 us -> 48.9 us
    all_to_all x2, blocking collectives: 50.3 us -> 48.9 us  [the longest x1 36.6 us: body(): received = lax.all_to_all(run_turn(in_plane), 'z', 0, 0, tiled=True)]
where the time goes in v3:
time: 83.7 us; the launch traced here: 83.4 us
  blocking collectives  48.9 us (58%)
  starting transfers between devices  27.1 us (32%)
  Pallas kernels  6.25 us (7%)
  local copies, waits for them, and re-layouts  1.06 us (1%)
    all_to_all x1, blocking collectives, body(): received = lax.all_to_all(run_turn(in_plane), 'z', 0, 0, tiled=True)  36.6 us
    ppermute x1, starting transfers between devices, body(): face_y = lax.ppermute(face_y, ('z', 'c'), next_y)  16.3 us
    all_to_all x1, blocking collectives, body(): in_plane = lax.all_to_all(send, ('gz', 'c'), 0, 0, tiled=True)  12.4 us
    ppermute x1, starting transfers between devices, body(): edge = lax.ppermute(edge, ('gz', 'z', 'c'), next_zy)  8.35 us
    pallas_call x1, Pallas kernels, run_inner(): pl.pallas_call(inner_kernel, out_shape=(jax.ShapeDtypeStruct((8, num_rows...  3.37 us
    ppermute x1, starting transfers between devices, body(): face_z = lax.ppermute(face_z, 'gz', next_z)  2.37 us
  transfers between devices with their start and end apart: 3, of which 0 were waited for; matrix products, arithmetic and copies ran while one was open for 0% of the time, Pallas kernels for 4%

profile of v3, /device:TPU:1, one launch (start us, length us, event | category | flops | bytes accessed | tf_op | source)
XLA Modules:
  0.0 83.4 jit_solution(6245383091539738290)
XLA Ops:
  0.0 0.0 copy-start
  0.0 1.0 %copy-done = f32[16,16,512]{2,1,0:T(8,128)S(1)} copy-done((f32[16,16,512]{2,1,0:T(8,128)S(1)}, f32[16,16,512]{2,1,0:T(8,128)}, u32[]{:S(2)}) %copy-start) | copy-done | bytes 524312
  1.0 0.0 copy-start.1
  1.0 0.0 copy-start.2
  1.0 0.0 copy-start.3
  1.1 8.3 %collective-permute-start.2 = (f32[1,512]{1,0:T(1,128)S(1)}, f32[1,512]{1,0:T(1,128)S(1)}, u32[]{:S(2)}, u32[]{:S(2)}) collective-permute-start(f32[1,512]{1,0:T(1,128)S(1)} %get-tuple-element.12), channel_id=1, source_target_pairs={{65,0},{66,1},{67,2},{68,3},{69,4},{70,5},{71,6},{72,7},{73,8},{74... | collective-permute-start | bytes 6152 | tf_op jit(solution)/shard_map/ppermute | solution.py:277
  9.4 2.4 %collective-permute-start = (f32[16,512]{1,0:T(8,128)S(1)}, f32[16,512]{1,0:T(8,128)S(1)}, u32[]{:S(2)}, u32[]{:S(2)}) collective-permute-start(f32[16,512]{1,0:T(8,128)S(1)} %get-tuple-element.10), channel_id=1, source_target_pairs={{64,0},{128,64},{192,128},{256,192},{320,256},{384,320},{448,384},... | collective-permute-start | bytes 98312 | tf_op jit(solution)/shard_map/ppermute | solution.py:275
  11.8 16.3 %collective-permute-start.1 = (f32[16,512]{1,0:T(8,128)S(1)}, f32[16,512]{1,0:T(8,128)S(1)}, u32[]{:S(2)}, u32[]{:S(2)}) collective-permute-start(f32[16,512]{1,0:T(8,128)S(1)} %get-tuple-element.11), channel_id=1, source_target_pairs={{1,0},{2,1},{3,2},{4,3},{5,4},{6,5},{7,6},{8,7},{9,8},{10,9},{11,1... | collective-permute-start | bytes 98312 | tf_op jit(solution)/shard_map/ppermute | solution.py:276
  28.1 0.0 copy-done.1
  28.1 0.0 copy-done.2
  28.1 0.0 copy-done.3
  28.1 0.0 copy-start.4
  28.1 3.4 %inner.1 = (f32[8,2048]{1,0:T(8,128)S(1)}, s32[1,2048]{1,0:T(1,128)S(1)}) custom-call(f32[256,512]{1,0:T(8,128)S(1)} %bitcast.8, s32[3,2048]{1,0:T(4,128)S(1)} %copy-done.1, s32[3,2048]{1,0:T(4,128)S(1)} %copy-done.2, s32[1,2048]{1,0:T(1,128)S(1)} %bitcast.13), custom_call_target="tpu_custom_call" | custom-call | flops 2147483648 | bytes 1000000 | tf_op jit(solution)/shard_map/inner/pallas_call | solution.py:214
  31.5 0.0 collective-permute-done.2.edge_ref
  31.5 0.0 collective-permute-done.face_z_ref
  31.5 0.0 collective-permute-done.1.face_y_ref
  31.6 0.0 copy-done.4
  31.6 1.2 %send.1 = f32[128,128]{1,0:T(8,128)S(1)} custom-call(f32[16,512]{1,0:T(8,128)S(1)} %collective-permute-done.face_z_ref, f32[16,512]{1,0:T(8,128)S(1)} %collective-permute-done.1.face_y_ref, f32[1,512]{1,0:T(1,128)S(1)} %collective-permute-done.2.edge_ref, f32[8,2048]{1,0:T(8,128)S(1)} %get-tuple-element.13.grad_ref, ...), custom_call_target="tpu_custom_call" | custom-call | tf_op jit(solution)/shard_map/send/pallas_call | solution.py:231
  32.8 12.4 %all_to_all.22 = f32[32,4,128]{2,1,0:T(4,128)S(1)} all-to-all(f32[32,4,128]{2,1,0:T(4,128)S(1)} %bitcast.12), channel_id=1, replica_groups=mesh['gz'=16,'z'=32,'c'=2] {'gz','c'}, dimensions={0} | all-to-all | bytes 131072 | tf_op jit(solution)/shard_map/all_to_all | solution.py:282
  45.2 0.1 turn.1
  45.3 36.6 %all_to_all.23 = f32[32,4,128]{2,1,0:T(4,128)S(1)} all-to-all(f32[32,4,128]{2,1,0:T(4,128)S(1)} %bitcast.10), channel_id=1, replica_groups=mesh['gz'=16,'z'=32,'c'=2] {'z'}, dimensions={0} | all-to-all | bytes 131072 | tf_op jit(solution)/shard_map/all_to_all | solution.py:283
  81.8 1.6 %place.1 = f32[3,2048]{1,0:T(4,128)} custom-call(f32[128,128]{1,0:T(8,128)S(1)} %bitcast.11), custom_call_target="tpu_custom_call" | custom-call | tf_op jit(solution)/shard_map/place/pallas_call | solution.py:254
  (1 shorter events, 0.0 us)
Async XLA Ops:
  0.0 1.0 %copy-start = (f32[16,16,512]{2,1,0:T(8,128)S(1)}, f32[16,16,512]{2,1,0:T(8,128)}, u32[]{:S(2)}) copy-start(f32[16,16,512]{2,1,0:T(8,128)} %param.5) | copy-start | bytes 1572868
  1.0 27.1 %copy-start.1 = (s32[3,2048]{1,0:T(4,128)S(1)}, s32[3,2048]{1,0:T(4,128)}, u32[]{:S(2)}) copy-start(s32[3,2048]{1,0:T(4,128)} %cells_ref.3) | copy-start | bytes 73732
  1.0 27.1 %copy-start.2 = (s32[3,2048]{1,0:T(4,128)S(1)}, s32[3,2048]{1,0:T(4,128)}, u32[]{:S(2)}) copy-start(s32[3,2048]{1,0:T(4,128)} %offsets_ref.3) | copy-start | bytes 73732
  1.0 27.1 %copy-start.3 = (s32[2048,1]{0,1:T(1,128)S(1)}, s32[2048,1]{0,1:T(1,128)}, u32[]{:S(2)}) copy-start(s32[2048,1]{0,1:T(1,128)} %param.8) | copy-start | bytes 24580
  1.1 30.5 %collective-permute-start.2 = (f32[1,512]{1,0:T(1,128)S(1)}, f32[1,512]{1,0:T(1,128)S(1)}, u32[]{:S(2)}, u32[]{:S(2)}) collective-permute-start(f32[1,512]{1,0:T(1,128)S(1)} %get-tuple-element.12), channel_id=1, source_target_pairs={{65,0},{66,1},{67,2},{68,3},{69,4},{70,5},{71,6},{72,7},{73,8},{74... | collective-permute-start | bytes 6152 | tf_op jit(solution)/shard_map/ppermute | solution.py:277
  9.4 22.1 %collective-permute-start = (f32[16,512]{1,0:T(8,128)S(1)}, f32[16,512]{1,0:T(8,128)S(1)}, u32[]{:S(2)}, u32[]{:S(2)}) collective-permute-start(f32[16,512]{1,0:T(8,128)S(1)} %get-tuple-element.10), channel_id=1, source_target_pairs={{64,0},{128,64},{192,128},{256,192},{320,256},{384,320},{448,384},... | collective-permute-start | bytes 98312 | tf_op jit(solution)/shard_map/ppermute | solution.py:275
  11.8 19.8 %collective-permute-start.1 = (f32[16,512]{1,0:T(8,128)S(1)}, f32[16,512]{1,0:T(8,128)S(1)}, u32[]{:S(2)}, u32[]{:S(2)}) collective-permute-start(f32[16,512]{1,0:T(8,128)S(1)} %get-tuple-element.11), channel_id=1, source_target_pairs={{1,0},{2,1},{3,2},{4,3},{5,4},{6,5},{7,6},{8,7},{9,8},{10,9},{11,1... | collective-permute-start | bytes 98312 | tf_op jit(solution)/shard_map/ppermute | solution.py:276
  28.1 3.4 %copy-start.4 = (s32[2048]{0:T(1024)S(1)}, s32[2048]{0:T(1024)}, u32[]{:S(2)}) copy-start(s32[2048]{0:T(1024)} %param.9) | copy-start | bytes 24580

commit v4 on v3

--- a/solution.py
+++ b/solution.py
@@ -16,12 +16,14 @@
     return high, (x - high.astype(F32)).astype(BF16)
 
 
-def hot(mask):
-    return jnp.where(mask, 1.0, 0.0).astype(BF16)
-
-
 def rows_of(shape):
     return lax.broadcasted_iota(jnp.int32, shape, 0)
+
+
+def hot_rows(shape, place):
+    narrow = jnp.broadcast_to(place.astype(jnp.int16), shape)
+    one = jnp.ones(shape, BF16)
+    return jnp.where(rows_of(shape).astype(jnp.int16) == narrow, one, jnp.zeros(shape, BF16))
 
 
 def lane_tile(ref, row, t):
@@ -74,7 +76,7 @@
 def read_tiles(lhs_ref, cells_ref, offsets_ref, grad_ref):
     rows, size_x = lhs_ref.shape[0] // 2, lhs_ref.shape[1] // 2
     for t in range(cells_ref.shape[1] // TILE):
-        at_x = hot(rows_of((size_x, TILE)) == lane_tile(cells_ref, 2, t))
+        at_x = hot_rows((size_x, TILE), lane_tile(cells_ref, 2, t))
         read = jnp.dot(lhs_ref[...], jnp.concatenate([at_x, at_x], 0), preferred_element_type=F32)
         frac = [fraction_of(lane_tile(offsets_ref, a, t)) for a in range(3)]
         index_z = jnp.broadcast_to(lane_tile(cells_ref, 0, t) & 15, (16, TILE))
@@ -127,7 +129,7 @@
             halo_ref[(2 * half + part) * count : (2 * half + part + 1) * count, :] = piece
     for t in range(cells_ref.shape[1] // TILE):
         lanes = slice(t * TILE, (t + 1) * TILE)
-        at_x = hot(rows_of((size_x, TILE)) == lane_tile(cells_ref, 2, t))
+        at_x = hot_rows((size_x, TILE), lane_tile(cells_ref, 2, t))
         read = jnp.dot(halo_ref[...], at_x, preferred_element_type=F32)
         read = read[: 2 * count] + read[2 * count :]
         frac = [fraction_of(lane_tile(offsets_ref, a, t)) for a in range(3)]
@@ -161,7 +163,7 @@
         for half, piece in enumerate(split(four)):
             tall = jnp.concatenate([piece.astype(F32)] * 16, 0)
             value_ref[half * 128 : (half + 1) * 128, lanes] = jnp.where(here, tall, 0.0).astype(BF16)
-        hot_ref[:, lanes] = hot(rows_of((128, TILE)) == place_ref[:, lanes])
+        hot_ref[:, lanes] = hot_rows((128, TILE), place_ref[:, lanes])
     both = lax.dot_general(
         value_ref[...], hot_ref[...], (((1,), (1,)), ((), ())), preferred_element_type=F32
     )
@@ -185,7 +187,7 @@
             eight = jnp.concatenate([four, four], 0)
             tall = jnp.concatenate([eight] * 8, 0)
             value_ref[half * 64 : (half + 1) * 64, lanes] = jnp.where(here, tall, 0.0).astype(BF16)
-        hot_ref[:, lanes] = hot(rows_of((128, 128)) == (slot & 127))
+        hot_ref[:, lanes] = hot_rows((128, 128), slot & 127)
     both = lax.dot_general(
         value_ref[...], hot_ref[...], (((1,), (1,)), ((), ())), preferred_element_type=F32
     )

time: 83.7 us -> 83.4 us (level)
  no operation moved by 1% of the time
where the time goes in v4:
time: 83.4 us; the launch traced here: 83.1 us
  blocking collectives  49.3 us (59%)
  starting transfers between devices  27.1 us (32%)
  Pallas kernels  5.57 us (7%)
  local copies, waits for them, and re-layouts  1.06 us (1%)
    all_to_all x1, blocking collectives, body(): received = lax.all_to_all(run_turn(in_plane), 'z', 0, 0, tiled=True)  36.6 us
    ppermute x1, starting transfers between devices, body(): face_y = lax.ppermute(face_y, ('z', 'c'), next_y)  16.3 us
    all_to_all x1, blocking collectives, body(): in_plane = lax.all_to_all(send, ('gz', 'c'), 0, 0, tiled=True)  12.7 us
    ppermute x1, starting transfers between devices, body(): edge = lax.ppermute(edge, ('gz', 'z', 'c'), next_zy)  8.35 us
    pallas_call x1, Pallas kernels, run_inner(): pl.pallas_call(inner_kernel, out_shape=(jax.ShapeDtypeStruct((8, num_rows...  3 us
    ppermute x1, starting transfers between devices, body(): face_z = lax.ppermute(face_z, 'gz', next_z)  2.37 us
  transfers between devices with their start and end apart: 3, of which 0 were waited for; matrix products, arithmetic and copies ran while one was open for 0% of the time, Pallas kernels for 4%

profile of v4, /device:TPU:1, one launch (start us, length us, event | category | flops | bytes accessed | tf_op | source)
XLA Modules:
  0.0 83.1 jit_solution(5177034049592236233)
XLA Ops:
  0.0 0.0 copy-start
  0.0 1.0 %copy-done = f32[16,16,512]{2,1,0:T(8,128)S(1)} copy-done((f32[16,16,512]{2,1,0:T(8,128)S(1)}, f32[16,16,512]{2,1,0:T(8,128)}, u32[]{:S(2)}) %copy-start) | copy-done | bytes 524312
  1.0 0.0 copy-start.1
  1.0 0.0 copy-start.2
  1.0 0.0 copy-start.3
  1.1 8.3 %collective-permute-start.2 = (f32[1,512]{1,0:T(1,128)S(1)}, f32[1,512]{1,0:T(1,128)S(1)}, u32[]{:S(2)}, u32[]{:S(2)}) collective-permute-start(f32[1,512]{1,0:T(1,128)S(1)} %get-tuple-element.12), channel_id=1, source_target_pairs={{65,0},{66,1},{67,2},{68,3},{69,4},{70,5},{71,6},{72,7},{73,8},{74... | collective-permute-start | bytes 6152 | tf_op jit(solution)/shard_map/ppermute | solution.py:279
  9.4 2.4 %collective-permute-start = (f32[16,512]{1,0:T(8,128)S(1)}, f32[16,512]{1,0:T(8,128)S(1)}, u32[]{:S(2)}, u32[]{:S(2)}) collective-permute-start(f32[16,512]{1,0:T(8,128)S(1)} %get-tuple-element.10), channel_id=1, source_target_pairs={{64,0},{128,64},{192,128},{256,192},{320,256},{384,320},{448,384},... | collective-permute-start | bytes 98312 | tf_op jit(solution)/shard_map/ppermute | solution.py:277
  11.8 16.3 %collective-permute-start.1 = (f32[16,512]{1,0:T(8,128)S(1)}, f32[16,512]{1,0:T(8,128)S(1)}, u32[]{:S(2)}, u32[]{:S(2)}) collective-permute-start(f32[16,512]{1,0:T(8,128)S(1)} %get-tuple-element.11), channel_id=1, source_target_pairs={{1,0},{2,1},{3,2},{4,3},{5,4},{6,5},{7,6},{8,7},{9,8},{10,9},{11,1... | collective-permute-start | bytes 98312 | tf_op jit(solution)/shard_map/ppermute | solution.py:278
  28.1 0.0 copy-done.1
  28.1 0.0 copy-done.2
  28.1 0.0 copy-done.3
  28.1 0.0 copy-start.4
  28.1 3.0 %inner.1 = (f32[8,2048]{1,0:T(8,128)S(1)}, s32[1,2048]{1,0:T(1,128)S(1)}) custom-call(f32[256,512]{1,0:T(8,128)S(1)} %bitcast.8, s32[3,2048]{1,0:T(4,128)S(1)} %copy-done.1, s32[3,2048]{1,0:T(4,128)S(1)} %copy-done.2, s32[1,2048]{1,0:T(1,128)S(1)} %bitcast.13), custom_call_target="tpu_custom_call" | custom-call | flops 2147483648 | bytes 1000000 | tf_op jit(solution)/shard_map/inner/pallas_call | solution.py:216
  31.2 0.0 collective-permute-done.2.edge_ref
  31.2 0.0 collective-permute-done.face_z_ref
  31.2 0.0 collective-permute-done.1.face_y_ref
  31.2 0.0 copy-done.4
  31.2 1.0 %send.1 = f32[128,128]{1,0:T(8,128)S(1)} custom-call(f32[16,512]{1,0:T(8,128)S(1)} %collective-permute-done.face_z_ref, f32[16,512]{1,0:T(8,128)S(1)} %collective-permute-done.1.face_y_ref, f32[1,512]{1,0:T(1,128)S(1)} %collective-permute-done.2.edge_ref, f32[8,2048]{1,0:T(8,128)S(1)} %get-tuple-element.13.grad_ref, ...), custom_call_target="tpu_custom_call" | custom-call | tf_op jit(solution)/shard_map/send/pallas_call | solution.py:233
  32.2 12.7 %all_to_all.22 = f32[32,4,128]{2,1,0:T(4,128)S(1)} all-to-all(f32[32,4,128]{2,1,0:T(4,128)S(1)} %bitcast.12), channel_id=1, replica_groups=mesh['gz'=16,'z'=32,'c'=2] {'gz','c'}, dimensions={0} | all-to-all | bytes 131072 | tf_op jit(solution)/shard_map/all_to_all | solution.py:284
  45.0 0.1 turn.1
  45.1 36.6 %all_to_all.23 = f32[32,4,128]{2,1,0:T(4,128)S(1)} all-to-all(f32[32,4,128]{2,1,0:T(4,128)S(1)} %bitcast.10), channel_id=1, replica_groups=mesh['gz'=16,'z'=32,'c'=2] {'z'}, dimensions={0} | all-to-all | bytes 131072 | tf_op jit(solution)/shard_map/all_to_all | solution.py:285
  81.7 1.5 %place.1 = f32[3,2048]{1,0:T(4,128)} custom-call(f32[128,128]{1,0:T(8,128)S(1)} %bitcast.11), custom_call_target="tpu_custom_call" | custom-call | tf_op jit(solution)/shard_map/place/pallas_call | solution.py:256
  (1 shorter events, 0.0 us)
Async XLA Ops:
  0.0 1.0 %copy-start = (f32[16,16,512]{2,1,0:T(8,128)S(1)}, f32[16,16,512]{2,1,0:T(8,128)}, u32[]{:S(2)}) copy-start(f32[16,16,512]{2,1,0:T(8,128)} %param.5) | copy-start | bytes 1572868
  1.0 27.1 %copy-start.1 = (s32[3,2048]{1,0:T(4,128)S(1)}, s32[3,2048]{1,0:T(4,128)}, u32[]{:S(2)}) copy-start(s32[3,2048]{1,0:T(4,128)} %cells_ref.3) | copy-start | bytes 73732
  1.0 27.1 %copy-start.2 = (s32[3,2048]{1,0:T(4,128)S(1)}, s32[3,2048]{1,0:T(4,128)}, u32[]{:S(2)}) copy-start(s32[3,2048]{1,0:T(4,128)} %offsets_ref.3) | copy-start | bytes 73732
  1.0 27.1 %copy-start.3 = (s32[2048,1]{0,1:T(1,128)S(1)}, s32[2048,1]{0,1:T(1,128)}, u32[]{:S(2)}) copy-start(s32[2048,1]{0,1:T(1,128)} %param.8) | copy-start | bytes 24580
  1.1 30.1 %collective-permute-start.2 = (f32[1,512]{1,0:T(1,128)S(1)}, f32[1,512]{1,0:T(1,128)S(1)}, u32[]{:S(2)}, u32[]{:S(2)}) collective-permute-start(f32[1,512]{1,0:T(1,128)S(1)} %get-tuple-element.12), channel_id=1, source_target_pairs={{65,0},{66,1},{67,2},{68,3},{69,4},{70,5},{71,6},{72,7},{73,8},{74... | collective-permute-start | bytes 6152 | tf_op jit(solution)/shard_map/ppermute | solution.py:279
  9.4 21.7 %collective-permute-start = (f32[16,512]{1,0:T(8,128)S(1)}, f32[16,512]{1,0:T(8,128)S(1)}, u32[]{:S(2)}, u32[]{:S(2)}) collective-permute-start(f32[16,512]{1,0:T(8,128)S(1)} %get-tuple-element.10), channel_id=1, source_target_pairs={{64,0},{128,64},{192,128},{256,192},{320,256},{384,320},{448,384},... | collective-permute-start | bytes 98312 | tf_op jit(solution)/shard_map/ppermute | solution.py:277
  11.8 19.4 %collective-permute-start.1 = (f32[16,512]{1,0:T(8,128)S(1)}, f32[16,512]{1,0:T(8,128)S(1)}, u32[]{:S(2)}, u32[]{:S(2)}) collective-permute-start(f32[16,512]{1,0:T(8,128)S(1)} %get-tuple-element.11), channel_id=1, source_target_pairs={{1,0},{2,1},{3,2},{4,3},{5,4},{6,5},{7,6},{8,7},{9,8},{10,9},{11,1... | collective-permute-start | bytes 98312 | tf_op jit(solution)/shard_map/ppermute | solution.py:278
  28.1 3.0 %copy-start.4 = (s32[2048]{0:T(1024)S(1)}, s32[2048]{0:T(1024)}, u32[]{:S(2)}) copy-start(s32[2048]{0:T(1024)} %param.9) | copy-start | bytes 24580

commit v5 on v4

--- a/solution.py
+++ b/solution.py
@@ -4,6 +4,7 @@
 from jax.experimental import pallas as pl
 from jax.experimental.pallas import tpu as pltpu
 from jax.sharding import Mesh, PartitionSpec as P
+
 
 F32 = jnp.float32
 BF16 = jnp.bfloat16
@@ -65,10 +66,13 @@
     return jnp.concatenate([jnp.sum(c, axis=0, keepdims=True) for c in counts], 1)
 
 
-def faces_kernel(grid_ref, face_z_ref, face_y_ref, edge_ref):
-    block_z, block_y = face_y_ref.shape[0], face_z_ref.shape[0]
-    face_z_ref[...] = grid_ref[:block_y]
-    edge_ref[...] = grid_ref[:1]
+def edge_kernel(face_z_ref, edge_ref):
+    edge_ref[...] = face_z_ref[:1]
+
+
+def face_y_kernel(grid_ref, face_y_ref):
+    block_z = face_y_ref.shape[0]
+    block_y = grid_ref.shape[0] // block_z
     for z in range(block_z):
         face_y_ref[z : z + 1] = grid_ref[z * block_y : z * block_y + 1]
 
@@ -196,17 +200,21 @@
         out_ref[:, h * 128 : (h + 1) * 128] = total[4 * h : 4 * h + 3]
 
 
-def run_faces(plane, block_z, block_y):
-    size_x = plane.shape[1]
-    return pl.pallas_call(
-        faces_kernel,
-        out_shape=(
-            jax.ShapeDtypeStruct((block_y, size_x), F32),
-            jax.ShapeDtypeStruct((block_z, size_x), F32),
-            jax.ShapeDtypeStruct((1, size_x), F32),
-        ),
-        compiler_params=SMALL,
-        name="faces",
+def run_edge(face_z):
+    return pl.pallas_call(
+        edge_kernel,
+        out_shape=jax.ShapeDtypeStruct((1, face_z.shape[1]), F32),
+        compiler_params=SMALL,
+        name="edge",
+    )(face_z)
+
+
+def run_face_y(plane, block_z):
+    return pl.pallas_call(
+        face_y_kernel,
+        out_shape=jax.ShapeDtypeStruct((block_z, plane.shape[1]), F32),
+        compiler_params=SMALL,
+        name="face_y",
     )(plane)
 
 
@@ -273,7 +281,9 @@
         (sz * count_y + sy, dz * count_y + dy) for sz, dz in next_z for sy, dy in next_y
     ]
     plane = grid_grad.reshape(block_z * block_y, size_x)
-    face_z, face_y, edge = run_faces(plane, block_z, block_y)
+    face_z = grid_grad[0]
+    edge = run_edge(face_z)
+    face_y = run_face_y(plane, block_z)
     face_z = lax.ppermute(face_z, "gz", next_z)
     face_y = lax.ppermute(face_y, ("z", "c"), next_y)
     edge = lax.ppermute(edge, ("gz", "z", "c"), next_zy)

time: 83.4 us -> 82.7 us (level)
  blocking collectives: 49.3 us -> 48.2 us
    ppermute x1, starting transfers between devices: 2.37 us -> 7.64 us  [body(): face_z = lax.ppermute(face_z, 'gz', next_z)]
    ppermute x1, starting transfers between devices: 8.35 us -> 3.21 us  [body(): edge = lax.ppermute(edge, ('gz', 'z', 'c'), next_zy)]
    all_to_all x1, blocking collectives: 12.7 us -> 11.3 us  [body(): in_plane = lax.all_to_all(send, ('gz', 'c'), 0, 0, tiled=True)]
where the time goes in v5:
time: 82.7 us; the launch traced here: 82.3 us
  blocking collectives  48.2 us (58%)
  starting transfers between devices  26.6 us (32%)
  Pallas kernels  5.57 us (7%)
  local copies, waits for them, and re-layouts  1.81 us (2%)
    all_to_all x1, blocking collectives, body(): received = lax.all_to_all(run_turn(in_plane), 'z', 0, 0, tiled=True)  36.9 us
    ppermute x1, starting transfers between devices, body(): face_y = lax.ppermute(face_y, ('z', 'c'), next_y)  15.8 us
    all_to_all x1, blocking collectives, body(): in_plane = lax.all_to_all(send, ('gz', 'c'), 0, 0, tiled=True)  11.3 us
    ppermute x1, starting transfers between devices, body(): face_z = lax.ppermute(face_z, 'gz', next_z)  7.64 us
    ppermute x1, starting transfers between devices, body(): edge = lax.ppermute(edge, ('gz', 'z', 'c'), next_zy)  3.21 us
    pallas_call x1, Pallas kernels, run_inner(): pl.pallas_call(inner_kernel, out_shape=(jax.ShapeDtypeStruct((8, num_rows...  2.99 us
  transfers between devices with their start and end apart: 3, of which 0 were waited for; matrix products, arithmetic and copies ran while one was open for 0% of the time, Pallas kernels for 4%

profile of v5, /device:TPU:1, one launch (start us, length us, event | category | flops | bytes accessed | tf_op | source)
XLA Modules:
  0.0 82.3 jit_solution(17563543388973662054)
XLA Ops:
  0.0 0.8 slice_bitcast_fusion.face_z_ref
  0.8 7.6 %collective-permute-start = (f32[16,512]{1,0:T(8,128)S(1)}, f32[16,512]{1,0:T(8,128)S(1)}, u32[]{:S(2)}, u32[]{:S(2)}) collective-permute-start(f32[16,512]{1,0:T(8,128)S(1)} %slice_bitcast_fusion.face_z_ref), channel_id=1, source_target_pairs={{64,0},{128,64},{192,128},{256,192},{320,256},{384,320},{448,384},... | collective-permute-start | bytes 98312 | tf_op jit(solution)/shard_map/ppermute | solution.py:287
  8.4 3.2 %collective-permute-start.2 = (f32[1,512]{1,0:T(1,128)S(1)}, f32[1,512]{1,0:T(1,128)S(1)}, u32[]{:S(2)}, u32[]{:S(2)}) collective-permute-start(f32[1,512]{1,0:T(1,128)S(1)} %edge.1), channel_id=1, source_target_pairs={{65,0},{66,1},{67,2},{68,3},{69,4},{70,5},{71,6},{72,7},{73,8},{74... | collective-permute-start | bytes 6152 | tf_op jit(solution)/shard_map/ppermute | solution.py:289
  11.6 0.0 copy-start
  11.7 1.0 %copy-done = f32[16,16,512]{2,1,0:T(8,128)S(1)} copy-done((f32[16,16,512]{2,1,0:T(8,128)S(1)}, f32[16,16,512]{2,1,0:T(8,128)}, u32[]{:S(2)}) %copy-start) | copy-done | bytes 524312
  12.7 0.0 copy-start.1
  12.7 0.0 copy-start.2
  12.7 0.0 copy-start.3
  12.7 15.8 %collective-permute-start.1 = (f32[16,512]{1,0:T(8,128)S(1)}, f32[16,512]{1,0:T(8,128)S(1)}, u32[]{:S(2)}, u32[]{:S(2)}) collective-permute-start(f32[16,512]{1,0:T(8,128)S(1)} %face_y.1), channel_id=1, source_target_pairs={{1,0},{2,1},{3,2},{4,3},{5,4},{6,5},{7,6},{8,7},{9,8},{10,9},{11,1... | collective-permute-start | bytes 98312 | tf_op jit(solution)/shard_map/ppermute | solution.py:288
  28.5 0.0 copy-done.1
  28.5 0.0 copy-done.2
  28.5 0.0 copy-done.3
  28.5 0.0 copy-start.4
  28.5 3.0 %inner.1 = (f32[8,2048]{1,0:T(8,128)S(1)}, s32[1,2048]{1,0:T(1,128)S(1)}) custom-call(f32[256,512]{1,0:T(8,128)S(1)} %bitcast.10, s32[3,2048]{1,0:T(4,128)S(1)} %copy-done.1, s32[3,2048]{1,0:T(4,128)S(1)} %copy-done.2, s32[1,2048]{1,0:T(1,128)S(1)} %bitcast.15), custom_call_target="tpu_custom_call" | custom-call | flops 2147483648 | bytes 1000000 | tf_op jit(solution)/shard_map/inner/pallas_call | solution.py:224
  31.5 0.0 collective-permute-done.2.edge_ref
  31.5 0.0 collective-permute-done.1.face_y_ref
  31.5 0.0 collective-permute-done.face_z_ref
  31.5 0.0 copy-done.4
  31.5 1.0 %send.1 = f32[128,128]{1,0:T(8,128)S(1)} custom-call(f32[16,512]{1,0:T(8,128)S(1)} %collective-permute-done.face_z_ref, f32[16,512]{1,0:T(8,128)S(1)} %collective-permute-done.1.face_y_ref, f32[1,512]{1,0:T(1,128)S(1)} %collective-permute-done.2.edge_ref, f32[8,2048]{1,0:T(8,128)S(1)} %get-tuple-element.7.grad_ref, ...), custom_call_target="tpu_custom_call" | custom-call | tf_op jit(solution)/shard_map/send/pallas_call | solution.py:241
  32.6 11.3 %all_to_all.22 = f32[32,4,128]{2,1,0:T(4,128)S(1)} all-to-all(f32[32,4,128]{2,1,0:T(4,128)S(1)} %bitcast.14), channel_id=1, replica_groups=mesh['gz'=16,'z'=32,'c'=2] {'gz','c'}, dimensions={0} | all-to-all | bytes 131072 | tf_op jit(solution)/shard_map/all_to_all | solution.py:294
  43.9 0.1 turn.1
  44.0 36.9 %all_to_all.23 = f32[32,4,128]{2,1,0:T(4,128)S(1)} all-to-all(f32[32,4,128]{2,1,0:T(4,128)S(1)} %bitcast.12), channel_id=1, replica_groups=mesh['gz'=16,'z'=32,'c'=2] {'z'}, dimensions={0} | all-to-all | bytes 131072 | tf_op jit(solution)/shard_map/all_to_all | solution.py:295
  80.9 1.5 %place.1 = f32[3,2048]{1,0:T(4,128)} custom-call(f32[128,128]{1,0:T(8,128)S(1)} %bitcast.13), custom_call_target="tpu_custom_call" | custom-call | tf_op jit(solution)/shard_map/place/pallas_call | solution.py:264
  (2 shorter events, 0.0 us)
Async XLA Ops:
  0.8 30.8 %collective-permute-start = (f32[16,512]{1,0:T(8,128)S(1)}, f32[16,512]{1,0:T(8,128)S(1)}, u32[]{:S(2)}, u32[]{:S(2)}) collective-permute-start(f32[16,512]{1,0:T(8,128)S(1)} %slice_bitcast_fusion.face_z_ref), channel_id=1, source_target_pairs={{64,0},{128,64},{192,128},{256,192},{320,256},{384,320},{448,384},... | collective-permute-start | bytes 98312 | tf_op jit(solution)/shard_map/ppermute | solution.py:287
  8.4 23.1 %collective-permute-start.2 = (f32[1,512]{1,0:T(1,128)S(1)}, f32[1,512]{1,0:T(1,128)S(1)}, u32[]{:S(2)}, u32[]{:S(2)}) collective-permute-start(f32[1,512]{1,0:T(1,128)S(1)} %edge.1), channel_id=1, source_target_pairs={{65,0},{66,1},{67,2},{68,3},{69,4},{70,5},{71,6},{72,7},{73,8},{74... | collective-permute-start | bytes 6152 | tf_op jit(solution)/shard_map/ppermute | solution.py:289
  11.6 1.0 %copy-start = (f32[16,16,512]{2,1,0:T(8,128)S(1)}, f32[16,16,512]{2,1,0:T(8,128)}, u32[]{:S(2)}) copy-start(f32[16,16,512]{2,1,0:T(8,128)} %param.5) | copy-start | bytes 1572868
  12.7 15.8 %copy-start.1 = (s32[3,2048]{1,0:T(4,128)S(1)}, s32[3,2048]{1,0:T(4,128)}, u32[]{:S(2)}) copy-start(s32[3,2048]{1,0:T(4,128)} %cells_ref.3) | copy-start | bytes 73732
  12.7 15.8 %copy-start.2 = (s32[3,2048]{1,0:T(4,128)S(1)}, s32[3,2048]{1,0:T(4,128)}, u32[]{:S(2)}) copy-start(s32[3,2048]{1,0:T(4,128)} %offsets_ref.3) | copy-start | bytes 73732
  12.7 15.8 %copy-start.3 = (s32[2048,1]{0,1:T(1,128)S(1)}, s32[2048,1]{0,1:T(1,128)}, u32[]{:S(2)}) copy-start(s32[2048,1]{0,1:T(1,128)} %param.8) | copy-start | bytes 24580
  12.7 18.8 %collective-permute-start.1 = (f32[16,512]{1,0:T(8,128)S(1)}, f32[16,512]{1,0:T(8,128)S(1)}, u32[]{:S(2)}, u32[]{:S(2)}) collective-permute-start(f32[16,512]{1,0:T(8,128)S(1)} %face_y.1), channel_id=1, source_target_pairs={{1,0},{2,1},{3,2},{4,3},{5,4},{6,5},{7,6},{8,7},{9,8},{10,9},{11,1... | collective-permute-start | bytes 98312 | tf_op jit(solution)/shard_map/ppermute | solution.py:288
  28.5 3.0 %copy-start.4 = (s32[2048]{0:T(1024)S(1)}, s32[2048]{0:T(1024)}, u32[]{:S(2)}) copy-start(s32[2048]{0:T(1024)} %param.9) | copy-start | bytes 24580

commit v6 on v5

--- a/solution.py
+++ b/solution.py
@@ -109,20 +109,20 @@
         grad_ref[:, lanes] = jnp.concatenate(sums + [jnp.zeros((5, TILE), F32)], 0)
 
 
-def inner_kernel(grid_ref, cells_ref, offsets_ref, owners_ref, grad_ref, place_ref, lhs_ref):
+def inner_kernel(grid_ref, cells_ref, offsets_ref, owners_ref, grad_ref, hot_ref, lhs_ref):
     rows, size_x = grid_ref.shape
     for part, block in enumerate(with_next_x(grid_ref[...])):
         for half, piece in enumerate(split(block)):
             lhs_ref[part * rows : (part + 1) * rows, half * size_x : (half + 1) * size_x] = piece
     owners = owners_ref[...]
     rank = count_earlier(owners).astype(jnp.int32)
-    place_ref[...] = ((owners >> 1) & 31) * 4 + rank
+    hot_ref[...] = hot_rows(hot_ref.shape, ((owners >> 1) & 31) * 4 + rank)
     read_tiles(lhs_ref, cells_ref, offsets_ref, grad_ref)
 
 
 def send_kernel(
-    face_z_ref, face_y_ref, edge_ref, grad_ref, place_ref, cells_ref, offsets_ref, owners_ref,
-    slots_ref, send_ref, halo_ref, value_ref, hot_ref,
+    face_z_ref, face_y_ref, edge_ref, grad_ref, hot_ref, cells_ref, offsets_ref, owners_ref,
+    slots_ref, send_ref, halo_ref, value_ref,
 ):
     size_x = edge_ref.shape[1]
     edge = jnp.broadcast_to(edge_ref[...], (8, size_x))
@@ -167,7 +167,6 @@
         for half, piece in enumerate(split(four)):
             tall = jnp.concatenate([piece.astype(F32)] * 16, 0)
             value_ref[half * 128 : (half + 1) * 128, lanes] = jnp.where(here, tall, 0.0).astype(BF16)
-        hot_ref[:, lanes] = hot_rows((128, TILE), place_ref[:, lanes])
     both = lax.dot_general(
         value_ref[...], hot_ref[...], (((1,), (1,)), ((), ())), preferred_element_type=F32
     )
@@ -225,7 +224,7 @@
         inner_kernel,
         out_shape=(
             jax.ShapeDtypeStruct((8, num_rows), F32),
-            jax.ShapeDtypeStruct((1, num_rows), jnp.int32),
+            jax.ShapeDtypeStruct((128, num_rows), BF16),
         ),
         scratch_shapes=[pltpu.VMEM((2 * rows, 2 * size_x), BF16)],
         compiler_params=SMALL,
@@ -244,7 +243,6 @@
         scratch_shapes=[
             pltpu.VMEM((160, edge.shape[1]), BF16),
             pltpu.VMEM((256, num_rows), BF16),
-            pltpu.VMEM((128, num_rows), BF16),
         ],
         compiler_params=SMALL,
         name="send",

time: 82.7 us -> 82.7 us (level)
  no operation moved by 1% of the time
where the time goes in v6:
time: 82.7 us; the launch traced here: 82.3 us
  blocking collectives  48.1 us (58%)
  starting transfers between devices  26.6 us (32%)
  Pallas kernels  5.67 us (7%)
  local copies, waits for them, and re-layouts  1.81 us (2%)
    all_to_all x1, blocking collectives, body(): received = lax.all_to_all(run_turn(in_plane), 'z', 0, 0, tiled=True)  36.9 us
    ppermute x1, starting transfers between devices, body(): face_y = lax.ppermute(face_y, ('z', 'c'), next_y)  15.8 us
    all_to_all x1, blocking collectives, body(): in_plane = lax.all_to_all(send, ('gz', 'c'), 0, 0, tiled=True)  11.3 us
    ppermute x1, starting transfers between devices, body(): face_z = lax.ppermute(face_z, 'gz', next_z)  7.64 us
    ppermute x1, starting transfers between devices, body(): edge = lax.ppermute(edge, ('gz', 'z', 'c'), next_zy)  3.21 us
    pallas_call x1, Pallas kernels, run_inner(): pl.pallas_call(inner_kernel, out_shape=(jax.ShapeDtypeStruct((8, num_rows...  3.07 us
  transfers between devices with their start and end apart: 3, of which 0 were waited for; matrix products, arithmetic and copies ran while one was open for 0% of the time, Pallas kernels for 4%

profile of v6, /device:TPU:1, one launch (start us, length us, event | category | flops | bytes accessed | tf_op | source)
XLA Modules:
  0.0 82.3 jit_solution(790849959368497563)
XLA Ops:
  0.0 0.8 slice_bitcast_fusion.face_z_ref
  0.8 7.6 %collective-permute-start = (f32[16,512]{1,0:T(8,128)S(1)}, f32[16,512]{1,0:T(8,128)S(1)}, u32[]{:S(2)}, u32[]{:S(2)}) collective-permute-start(f32[16,512]{1,0:T(8,128)S(1)} %slice_bitcast_fusion.face_z_ref), channel_id=1, source_target_pairs={{64,0},{128,64},{192,128},{256,192},{320,256},{384,320},{448,384},... | collective-permute-start | bytes 98312 | tf_op jit(solution)/shard_map/ppermute | solution.py:285
  8.4 3.2 %collective-permute-start.2 = (f32[1,512]{1,0:T(1,128)S(1)}, f32[1,512]{1,0:T(1,128)S(1)}, u32[]{:S(2)}, u32[]{:S(2)}) collective-permute-start(f32[1,512]{1,0:T(1,128)S(1)} %edge.1), channel_id=1, source_target_pairs={{65,0},{66,1},{67,2},{68,3},{69,4},{70,5},{71,6},{72,7},{73,8},{74... | collective-permute-start | bytes 6152 | tf_op jit(solution)/shard_map/ppermute | solution.py:287
  11.6 0.0 copy-start
  11.7 1.0 %copy-done = f32[16,16,512]{2,1,0:T(8,128)S(1)} copy-done((f32[16,16,512]{2,1,0:T(8,128)S(1)}, f32[16,16,512]{2,1,0:T(8,128)}, u32[]{:S(2)}) %copy-start) | copy-done | bytes 524312
  12.7 0.0 copy-start.1
  12.7 0.0 copy-start.2
  12.7 0.0 copy-start.3
  12.7 15.8 %collective-permute-start.1 = (f32[16,512]{1,0:T(8,128)S(1)}, f32[16,512]{1,0:T(8,128)S(1)}, u32[]{:S(2)}, u32[]{:S(2)}) collective-permute-start(f32[16,512]{1,0:T(8,128)S(1)} %face_y.1), channel_id=1, source_target_pairs={{1,0},{2,1},{3,2},{4,3},{5,4},{6,5},{7,6},{8,7},{9,8},{10,9},{11,1... | collective-permute-start | bytes 98312 | tf_op jit(solution)/shard_map/ppermute | solution.py:286
  28.5 0.0 copy-done.1
  28.5 0.0 copy-done.2
  28.5 0.0 copy-done.3
  28.5 0.0 copy-start.4
  28.5 3.1 %inner.1 = (f32[8,2048]{1,0:T(8,128)S(1)}, bf16[128,2048]{1,0:T(8,128)(2,1)S(1)}) custom-call(f32[256,512]{1,0:T(8,128)S(1)} %bitcast.10, s32[3,2048]{1,0:T(4,128)S(1)} %copy-done.1, s32[3,2048]{1,0:T(4,128)S(1)} %copy-done.2, s32[1,2048]{1,0:T(1,128)S(1)} %bitcast.15), custom_call_target="tpu_custom_call" | custom-call | flops 2147483648 | bytes 1000000 | tf_op jit(solution)/shard_map/inner/pallas_call | solution.py:223
  31.6 0.0 collective-permute-done.2.edge_ref
  31.6 0.0 collective-permute-done.1.face_y_ref
  31.6 0.0 collective-permute-done.face_z_ref
  31.6 0.0 copy-done.4
  31.6 1.0 %send.1 = f32[128,128]{1,0:T(8,128)S(1)} custom-call(f32[16,512]{1,0:T(8,128)S(1)} %collective-permute-done.face_z_ref, f32[16,512]{1,0:T(8,128)S(1)} %collective-permute-done.1.face_y_ref, f32[1,512]{1,0:T(1,128)S(1)} %collective-permute-done.2.edge_ref, f32[8,2048]{1,0:T(8,128)S(1)} %get-tuple-element.7.grad_ref, ...), custom_call_target="tpu_custom_call" | custom-call | tf_op jit(solution)/shard_map/send/pallas_call | solution.py:240
  32.7 11.3 %all_to_all.22 = f32[32,4,128]{2,1,0:T(4,128)S(1)} all-to-all(f32[32,4,128]{2,1,0:T(4,128)S(1)} %bitcast.11), channel_id=1, replica_groups=mesh['gz'=16,'z'=32,'c'=2] {'gz','c'}, dimensions={0} | all-to-all | bytes 131072 | tf_op jit(solution)/shard_map/all_to_all | solution.py:292
  43.9 0.1 turn.1
  44.0 36.9 %all_to_all.23 = f32[32,4,128]{2,1,0:T(4,128)S(1)} all-to-all(f32[32,4,128]{2,1,0:T(4,128)S(1)} %bitcast.13), channel_id=1, replica_groups=mesh['gz'=16,'z'=32,'c'=2] {'z'}, dimensions={0} | all-to-all | bytes 131072 | tf_op jit(solution)/shard_map/all_to_all | solution.py:293
  80.9 1.5 %place.1 = f32[3,2048]{1,0:T(4,128)} custom-call(f32[128,128]{1,0:T(8,128)S(1)} %bitcast.14), custom_call_target="tpu_custom_call" | custom-call | tf_op jit(solution)/shard_map/place/pallas_call | solution.py:262
  (2 shorter events, 0.0 us)
Async XLA Ops:
  0.8 30.8 %collective-permute-start = (f32[16,512]{1,0:T(8,128)S(1)}, f32[16,512]{1,0:T(8,128)S(1)}, u32[]{:S(2)}, u32[]{:S(2)}) collective-permute-start(f32[16,512]{1,0:T(8,128)S(1)} %slice_bitcast_fusion.face_z_ref), channel_id=1, source_target_pairs={{64,0},{128,64},{192,128},{256,192},{320,256},{384,320},{448,384},... | collective-permute-start | bytes 98312 | tf_op jit(solution)/shard_map/ppermute | solution.py:285
  8.4 23.2 %collective-permute-start.2 = (f32[1,512]{1,0:T(1,128)S(1)}, f32[1,512]{1,0:T(1,128)S(1)}, u32[]{:S(2)}, u32[]{:S(2)}) collective-permute-start(f32[1,512]{1,0:T(1,128)S(1)} %edge.1), channel_id=1, source_target_pairs={{65,0},{66,1},{67,2},{68,3},{69,4},{70,5},{71,6},{72,7},{73,8},{74... | collective-permute-start | bytes 6152 | tf_op jit(solution)/shard_map/ppermute | solution.py:287
  11.6 1.0 %copy-start = (f32[16,16,512]{2,1,0:T(8,128)S(1)}, f32[16,16,512]{2,1,0:T(8,128)}, u32[]{:S(2)}) copy-start(f32[16,16,512]{2,1,0:T(8,128)} %param.5) | copy-start | bytes 1572868
  12.7 15.8 %copy-start.1 = (s32[3,2048]{1,0:T(4,128)S(1)}, s32[3,2048]{1,0:T(4,128)}, u32[]{:S(2)}) copy-start(s32[3,2048]{1,0:T(4,128)} %cells_ref.3) | copy-start | bytes 73732
  12.7 15.8 %copy-start.2 = (s32[3,2048]{1,0:T(4,128)S(1)}, s32[3,2048]{1,0:T(4,128)}, u32[]{:S(2)}) copy-start(s32[3,2048]{1,0:T(4,128)} %offsets_ref.3) | copy-start | bytes 73732
  12.7 15.8 %copy-start.3 = (s32[2048,1]{0,1:T(1,128)S(1)}, s32[2048,1]{0,1:T(1,128)}, u32[]{:S(2)}) copy-start(s32[2048,1]{0,1:T(1,128)} %param.8) | copy-start | bytes 24580
  12.7 18.9 %collective-permute-start.1 = (f32[16,512]{1,0:T(8,128)S(1)}, f32[16,512]{1,0:T(8,128)S(1)}, u32[]{:S(2)}, u32[]{:S(2)}) collective-permute-start(f32[16,512]{1,0:T(8,128)S(1)} %face_y.1), channel_id=1, source_target_pairs={{1,0},{2,1},{3,2},{4,3},{5,4},{6,5},{7,6},{8,7},{9,8},{10,9},{11,1... | collective-permute-start | bytes 98312 | tf_op jit(solution)/shard_map/ppermute | solution.py:286
  28.5 3.1 %copy-start.4 = (s32[2048]{0:T(1024)S(1)}, s32[2048]{0:T(1024)}, u32[]{:S(2)}) copy-start(s32[2048]{0:T(1024)} %param.9) | copy-start | bytes 24580
